TPU v7x, 32 devices: a whole 2x2x4 slice. The times are simulated.
32 devices in a mesh: bump: 4 (over y, core), nx: 2 (over x), ny: 4 (over z).
Axes of the slice: x: 2, y: 2, z: 4, core: 2. Of those that a mesh axis runs over, the one named last changes fastest.
Arguments:
- payoff: float32 [262144], P(('nx', 'ny')), may hold values from -6 to 6
- positions: float32 [262144], P(('nx', 'ny')), may hold values from -20 to 20
- tables: float32 [8, 5, 262144], P('bump', None, ('nx', 'ny')), may hold values from 0.02 to 1, as said below
- offsets: int32 [8, 1024], P(None, ('nx', 'ny')), may hold values from -1 to 1
- vol_curve: float32 [8], replicated, may hold values from 0.5 to 1.2
- bucket: int32 [64], P('bump'), may hold values from 0 to 7
- bump_size: float32 [64], P('bump'), may hold values from 0.1 to 0.4
Outputs:
- bumped_values: float32 [64, 262144], P('bump', ('nx', 'ny'))
- vega: float32 [64], P('bump')
Inputs may be any that keep to these rules, and one draw needn't show every extreme that they name: `tables`: component 0 lies in [0.9, 1], components 1 and 3 in [0.1, 0.2], components 2 and 4 in [0.02, 0.06].
All inputs are finite; a program needn't handle non-finite values.
Results may differ from a plain program's by a relative error of at most 0.0003.
Values sent between devices are 32-bit elements; how exact they have to be, the bound alone decides.
A program may use at most 64 MiB of HBM per device.

v0:
```python
import functools

import jax
import jax.numpy as jnp
from jax import lax
from jax.experimental import pallas as pl
from jax.experimental.pallas import tpu as pltpu
from jax.sharding import PartitionSpec as P

LANES = 128
SUB = 8
MESH = pl.DeviceIdType.MESH


def sweep_kernel(
    dims,
    vol_ref,
    payoff_ref,
    positions_ref,
    offsets_ref,
    tables_ref,
    rows_ref,
    sums_ref,
    tab,
    pay,
    offs,
    kmask,
    state,
    part,
    part2,
    tab_send,
    tab_recv,
    nb_send,
    nb_recv,
    own_sem,
    res_send,
    res_recv,
    ring_send,
    ring_recv,
    grp_send,
    grp_recv,
):
    n, nx, ny, steps, per, block_len, chunks = dims
    ring_size = nx * ny
    rows = payoff_ref.shape[0]
    quarter = rows // n
    ext = quarter + 2 * SUB
    span = quarter // chunks
    wide = span + 2 * SUB
    me = lax.axis_index("bump")
    ring = lax.axis_index("nx") * ny + lax.axis_index("ny")

    def at(r, q):
        return {"bump": q, "nx": r // ny, "ny": r % ny}

    right = lax.rem(ring + 1, ring_size)
    left = lax.rem(ring + ring_size - 1, ring_size)

    barrier = pltpu.get_barrier_semaphore()
    peers = [at(ring, lax.rem(me + i, n)) for i in range(1, n)]
    peers += [at(lax.rem(ring + i, ring_size), me) for i in range(1, ring_size)]
    peers += [at(r, lax.rem(me + i, n)) for i in range(1, n) for r in (left, right)]
    for peer in peers:
        pl.semaphore_signal(barrier, inc=1, device_id=peer, device_id_type=MESH)
    pl.semaphore_wait(barrier, len(peers))

    def neighbour(i, src, dst, to):
        return pltpu.make_async_remote_copy(
            src_ref=src,
            dst_ref=dst,
            send_sem=nb_send.at[i],
            recv_sem=nb_recv.at[i],
            device_id=at(to, me),
            device_id_type=MESH,
        )

    near = [
        neighbour(0, payoff_ref.at[rows - SUB : rows], pay.at[0:SUB], right),
        neighbour(1, payoff_ref.at[0:SUB], pay.at[SUB + rows : SUB + rows + SUB], left),
        neighbour(2, offsets_ref, offs.at[0], right),
        neighbour(3, offsets_ref, offs.at[1], left),
    ]
    for copy in near:
        copy.start()

    last = chunks + 1

    def piece(kind, q):
        if kind == 0:
            source = slice((q + 1) * quarter - 1, (q + 1) * quarter)
            target = (q + 1) % n
            return target, (right if q == n - 1 else ring), source, slice(SUB - 1, SUB)
        if kind == last:
            source = slice(q * quarter, q * quarter + 1)
            target = (q - 1) % n
            landing = slice(SUB + quarter, SUB + quarter + 1)
            return target, (left if q == 0 else ring), source, landing
        lo = 0 if kind == 1 else (kind - 1) * span + SUB
        hi = quarter if kind == chunks else kind * span + SUB
        source = slice(q * quarter + lo, q * quarter + hi)
        return q, ring, source, slice(SUB + lo, SUB + hi)

    def table_copy(kind, q):
        target, at_ring, source, landing = piece(kind, q)
        crosses = (kind == 0 and q == n - 1) or (kind == last and q == 0)
        src = tables_ref.at[:, source]
        dst = tab.at[me, :, landing]

        def remote():
            return pltpu.make_async_remote_copy(
                src_ref=src,
                dst_ref=dst,
                send_sem=tab_send.at[kind, q],
                recv_sem=tab_recv.at[kind, me],
                device_id=at(at_ring, target),
                device_id_type=MESH,
            )

        def local():
            return pltpu.make_async_copy(src, dst, tab_recv.at[kind, me])

        return target, crosses, remote, local

    for kind in range(last + 1):
        for q in range(n):
            target, crosses, remote, local = table_copy(kind, q)
            if crosses:
                remote().start()
            else:
                pl.when(me != target)(lambda: remote().start())
                pl.when(me == target)(lambda: local().start())

    own = pltpu.make_async_copy(payoff_ref, pay.at[SUB : SUB + rows], own_sem)
    own.start()
    for copy in near:
        copy.wait()
    own.wait()

    blocks = offsets_ref.shape[1]
    rows_per_block = block_len // LANES
    row_at = lax.broadcasted_iota(jnp.int32, (ext, blocks), 0) + me * quarter
    row_at = row_at + (rows - SUB)
    block_at = row_at // rows_per_block - blocks
    lane_at = lax.broadcasted_iota(jnp.int32, (ext, blocks), 1)
    for s in range(steps):
        def spread(line, shift):
            hit = lane_at == block_at + shift
            return jnp.where(hit, line.astype(jnp.float32), 0.0)

        picked = (
            spread(offsets_ref[s : s + 1, :], 0)
            + spread(offs[0, s : s + 1, :], blocks)
            + spread(offs[1, s : s + 1, :], -blocks)
        )
        branch = jnp.sum(picked, axis=1, keepdims=True)
        kmask[s] = jnp.broadcast_to(branch, (ext, LANES))

    lane = lax.broadcasted_iota(jnp.int32, (wide, LANES), 1)

    def waits(kind, src):
        _, _, source, landing = piece(kind, 0)
        dst = tab.at[src, :, landing]
        pltpu.make_async_copy(tables_ref.at[:, source], dst, tab_recv.at[kind, src]).wait()

    def shifts(x):
        f1 = pltpu.roll(x, LANES - 1, 1)
        f2 = pltpu.roll(x, LANES - 2, 1)
        b1 = pltpu.roll(x, 1, 1)
        b2 = pltpu.roll(x, 2, 1)
        f1 = jnp.where(lane >= LANES - 1, pltpu.roll(f1, wide - 1, 0), f1)
        f2 = jnp.where(lane >= LANES - 2, pltpu.roll(f2, wide - 1, 0), f2)
        b1 = jnp.where(lane < 1, pltpu.roll(b1, 1, 0), b1)
        b2 = jnp.where(lane < 2, pltpu.roll(b2, 1, 0), b2)
        return b2, b1, f1, f2

    def roll_back(h):
        window = slice(h * span, h * span + wide)
        state[0] = pay[pl.ds(pl.multiple_of(me * quarter + h * span, SUB), wide), :]
        for s in reversed(range(steps)):
            src, step = s // per, s % per
            if step == per - 1:
                if h == 0:
                    waits(0, src)
                waits(h + 1, src)
                if h == chunks - 1:
                    waits(last, src)
            w = vol_ref[s] * vol_ref[s]
            discount = tab[src, 0, window, step, :]
            slope_up = discount * tab[src, 2, window, step, :]
            slope_down = discount * tab[src, 4, window, step, :]
            up = discount * tab[src, 1, window, step, :] + w * slope_up
            down = discount * tab[src, 3, window, step, :] + w * slope_down
            middle = discount - up - down
            branch = kmask[s, window]
            low = branch < -0.5
            high = branch > 0.5
            for g in [0] + list(range(s + 2, steps + 1)):
                x = state[g]
                b2, b1, f1, f2 = shifts(x)
                above = jnp.where(low, x, jnp.where(high, f2, f1))
                level = jnp.where(low, b1, jnp.where(high, f1, x))
                below = jnp.where(low, b2, jnp.where(high, x, b1))
                state[g] = up * above + middle * level + down * below
                if g == 0:
                    state[s + 1] = slope_up * (above - level) + slope_down * (below - level)
        here = pl.ds(pl.multiple_of(me * quarter + h * span, SUB), span)
        weights = positions_ref[here, :]
        for g in range(steps + 1):
            center = state[g, SUB : SUB + span, :]
            rows_ref[g, here, :] = center
            if g:
                weighted = jnp.sum(weights * center, axis=0, keepdims=True)
                if h:
                    weighted = weighted + part2[me, g - 1 : g, :]
                part2[me, g - 1 : g, :] = weighted

    def result(m, d, slot, h):
        first = jnp.bitwise_xor(me, m) * quarter + h * span
        held = pl.ds(pl.multiple_of(first, SUB), span)
        return pltpu.make_async_remote_copy(
            src_ref=rows_ref.at[:, held, :],
            dst_ref=rows_ref.at[:, held, :],
            send_sem=res_send.at[slot, h],
            recv_sem=res_recv.at[slot, h],
            device_id=at(ring, jnp.bitwise_xor(me, d)),
            device_id_type=MESH,
        )

    plan = []
    masks = [0]
    d = n // 2
    while d:
        plan += [(m, d) for m in masks]
        masks = masks + [m | d for m in masks]
        d //= 2
    slots = {m | d: i for i, (m, d) in enumerate(plan)}
    landed = set()
    copies = [[result(m, d, i, h) for h in range(chunks)] for i, (m, d) in enumerate(plan)]
    grp_copies = []
    for i in range(1, n):
        grp_copies.append(
            pltpu.make_async_remote_copy(
                src_ref=part2.at[me],
                dst_ref=part2.at[me],
                send_sem=grp_send.at[i],
                recv_sem=grp_recv.at[i],
                device_id=at(ring, lax.rem(me + i, n)),
                device_id_type=MESH,
            )
        )
    ring_copies = []
    for i in range(1, ring_size):
        ring_copies.append(
            pltpu.make_async_remote_copy(
                src_ref=part.at[ring],
                dst_ref=part.at[ring],
                send_sem=ring_send.at[i],
                recv_sem=ring_recv.at[i],
                device_id=at(lax.rem(ring + i, ring_size), me),
                device_id_type=MESH,
            )
        )

    def forward(h):
        for i, (m, d) in enumerate(plan):
            if m != 0:
                if (m, h) not in landed:
                    landed.add((m, h))
                    copies[slots[m]][h].wait_recv()
                copies[i][h].start()

    for h in range(chunks):
        roll_back(h)
        if h == chunks - 1:
            for copy in grp_copies:
                copy.start()
        for i, (m, d) in enumerate(plan):
            if m == 0:
                copies[i][h].start()
    for i in range(1, n):
        src = lax.rem(me + n - i, n)
        pltpu.make_async_copy(part2.at[src], part2.at[src], grp_recv.at[i]).wait()
    part[ring] = jnp.sum(part2[...], axis=0)
    for copy in ring_copies:
        copy.start()
    for h in range(chunks):
        forward(h)
    for i in range(1, ring_size):
        src = lax.rem(ring + ring_size - i, ring_size)
        pltpu.make_async_copy(part.at[src], part.at[src], ring_recv.at[i]).wait()
    sums_ref[...] = jnp.sum(part[...], axis=0)
    for copy in grp_copies + ring_copies:
        copy.wait_send()
    for h in range(chunks):
        for i, (m, d) in enumerate(plan):
            copies[i][h].wait_send()
            if (m | d, h) not in landed:
                copies[i][h].wait_recv()
    for kind in range(last + 1):
        for q in range(n):
            target, crosses, remote, _ = table_copy(kind, q)
            if crosses:
                remote().wait_send()
            else:
                pl.when(me != target)(lambda: remote().wait_send())


def spread_kernel(vol_ref, bucket_ref, bump_ref, rows_ref, sums_ref, out_ref, vega_ref):
    curves = bucket_ref.shape[0]
    base = rows_ref[0]
    for b in range(curves):
        s = bucket_ref[b]
        change = bump_ref[b] * (2.0 * vol_ref[s] + bump_ref[b])
        out_ref[b // SUB, :, b % SUB, :] = base + change * rows_ref[s + 1]

    @pl.when(pl.program_id(0) == 0)
    def _():
        lane = lax.broadcasted_iota(jnp.int32, (1, curves), 1)
        total = jnp.zeros((1, curves), jnp.float32)
        for b in range(curves):
            s = bucket_ref[b]
            slope = 2.0 * vol_ref[s] + bump_ref[b]
            weighted = jnp.sum(sums_ref[pl.ds(s, 1), :], axis=1, keepdims=True)
            total = jnp.where(lane == b, slope * weighted, total)
        vega_ref[...] = total


def on_device(n, nx, ny, payoff, positions, tables, offsets, vol_curve, bucket, bump_size):
    steps = vol_curve.shape[0]
    per, comps, nodes = tables.shape
    curves = bucket.shape[0]
    rows = nodes // LANES
    block_len = nodes // offsets.shape[1]
    quarter = rows // n
    ext = quarter + 2 * SUB
    ring = nx * ny
    chunks = 2
    wide = quarter // chunks + 2 * SUB
    tiles = tables.transpose(1, 0, 2).reshape(comps, per, rows, LANES).transpose(0, 2, 1, 3)
    dma = pltpu.SemaphoreType.DMA
    vmem = pl.BlockSpec(memory_space=pltpu.VMEM)
    smem = pl.BlockSpec(memory_space=pltpu.SMEM)
    moved, sums = pl.pallas_call(
        functools.partial(sweep_kernel, (n, nx, ny, steps, per, block_len, chunks)),
        out_shape=(
            jax.ShapeDtypeStruct((steps + 1, rows, LANES), jnp.float32),
            jax.ShapeDtypeStruct((steps, LANES), jnp.float32),
        ),
        in_specs=[smem, vmem, vmem, vmem, pl.BlockSpec(memory_space=pl.ANY)],
        out_specs=(vmem, vmem),
        scratch_shapes=[
            pltpu.VMEM((n, comps, ext, per, LANES), jnp.float32),
            pltpu.VMEM((rows + 2 * SUB, LANES), jnp.float32),
            pltpu.VMEM((2,) + offsets.shape, jnp.int32),
            pltpu.VMEM((steps, ext, LANES), jnp.float32),
            pltpu.VMEM((steps + 1, wide, LANES), jnp.float32),
            pltpu.VMEM((ring, steps, LANES), jnp.float32),
            pltpu.VMEM((n, steps, LANES), jnp.float32),
            dma((chunks + 2, n)),
            dma((chunks + 2, n)),
            dma((4,)),
            dma((4,)),
            dma,
            dma((n - 1, chunks)),
            dma((n - 1, chunks)),
            dma((ring,)),
            dma((ring,)),
            dma((n,)),
            dma((n,)),
        ],
        compiler_params=pltpu.CompilerParams(has_side_effects=True, collective_id=0),
        name="sweep",
    )(
        vol_curve,
        payoff.reshape(rows, LANES),
        positions.reshape(rows, LANES),
        offsets,
        tiles,
    )
    grid = max(1, n // 2)
    groups = curves // SUB
    bumped, vega = pl.pallas_call(
        spread_kernel,
        grid=(grid,),
        out_shape=(
            jax.ShapeDtypeStruct((groups, rows, SUB, LANES), jnp.float32),
            jax.ShapeDtypeStruct((1, curves), jnp.float32),
        ),
        in_specs=[
            smem,
            smem,
            smem,
            pl.BlockSpec((steps + 1, rows // grid, LANES), lambda i: (0, i, 0)),
            pl.BlockSpec((steps, LANES), lambda i: (0, 0)),
        ],
        out_specs=(
            pl.BlockSpec((groups, rows // grid, SUB, LANES), lambda i: (0, i, 0, 0)),
            pl.BlockSpec((1, curves), lambda i: (0, 0)),
        ),
        name="spread",
    )(vol_curve, bucket, bump_size, moved, sums)
    bumped = bumped.transpose(0, 2, 1, 3).reshape(curves, nodes)
    return bumped, vega.reshape(curves)


def solution(mesh):
    shape = dict(mesh.shape)
    in_specs = (
        P(("nx", "ny")),
        P(("nx", "ny")),
        P("bump", None, ("nx", "ny")),
        P(None, ("nx", "ny")),
        P(),
        P("bump"),
        P("bump"),
    )
    out_specs = (P("bump", ("nx", "ny")), P("bump"))
    body = functools.partial(on_device, shape["bump"], shape["nx"], shape["ny"])
    return jax.shard_map(body, mesh=mesh, in_specs=in_specs, out_specs=out_specs, check_vma=False)
```

profile of v0, /device:TPU:5, one launch (start us, length us, event | category | flops | bytes accessed | tf_op | source)
XLA Modules:
  0.0 37.1 jit_solution(17577216705369758722)
XLA Ops:
  0.6 33.0 %sweep.1 = (f32[9,256,128]{2,1,0:T(8,128)}, f32[8,128]{1,0:T(8,128)}) custom-call(f32[8]{0:T(128)} %vol_ref.3, f32[256,128]{1,0:T(8,128)} %bitcast.12, f32[256,128]{1,0:T(8,128)} %bitcast.13, s32[8,128]{1,0:T(8,128)} %offsets_ref.1, f32[5,256,2,128]{3,2,1,0:T(2,128)} %bitcast.11), custom_call_target="tpu_custom_call" | custom-call | tf_op jit(solution)/shard_map/sweep/pallas_call | solution.py:343
  33.6 3.5 %spread.1 = (f32[2,256,8,128]{3,2,1,0:T(8,128)}, f32[1,16]{1,0:T(1,128)}) custom-call(f32[8]{0:T(128)} %vol_ref.3, s32[16]{0:T(128)} %bucket_ref.1, f32[16]{0:T(128)} %bump_ref.1, f32[9,256,128]{2,1,0:T(8,128)} %get-tuple-element.6.rows_ref, f32[8,128]{1,0:T(8,128)} %get-tuple-element.7.sums_ref), custom_call_target="tpu_custom_call" | custom-call | tf_op jit(solution)/shard_map/spread/pallas_call | solution.py:382
where the time goes:
time: 37.8 us; the launch traced here: 37.1 us
  Pallas kernels  36.5 us (97%)
  between operations  0.64 us (2%)
    pallas_call x1, Pallas kernels, on_device(): pl.pallas_call(functools.partial(sweep_kernel, (n, nx, ny, steps, per, bl...  33 us
    pallas_call x1, Pallas kernels, on_device(): pl.pallas_call(spread_kernel, grid=(grid,), out_shape=(jax.ShapeDtypeStru...  3.5 us

commit v1 on v0

--- a/solution.py
+++ b/solution.py
@@ -9,6 +9,7 @@
 
 LANES = 128
 SUB = 8
+VMEM_LIMIT = 24 * 1024 * 1024
 MESH = pl.DeviceIdType.MESH
 
 
@@ -305,24 +306,35 @@
                 pl.when(me != target)(lambda: remote().wait_send())
 
 
-def spread_kernel(vol_ref, bucket_ref, bump_ref, rows_ref, sums_ref, out_ref, vega_ref):
+def spread_kernel(vol_ref, bucket_ref, bump_ref, rows_ref, sums_ref, out_ref, vega_ref, held, sem):
     curves = bucket_ref.shape[0]
-    base = rows_ref[0]
+    rows = rows_ref.shape[1]
+    parts = sem.shape[0]
+    span = rows // parts
+    picks = []
     for b in range(curves):
         s = bucket_ref[b]
-        change = bump_ref[b] * (2.0 * vol_ref[s] + bump_ref[b])
-        out_ref[b // SUB, :, b % SUB, :] = base + change * rows_ref[s + 1]
-
-    @pl.when(pl.program_id(0) == 0)
-    def _():
-        lane = lax.broadcasted_iota(jnp.int32, (1, curves), 1)
-        total = jnp.zeros((1, curves), jnp.float32)
+        slope = 2.0 * vol_ref[s] + bump_ref[b]
+        picks.append((s, slope, bump_ref[b] * slope))
+    copies = []
+    for i in range(parts):
+        here = slice(i * span, (i + 1) * span)
+        base = rows_ref[0, here, :]
         for b in range(curves):
-            s = bucket_ref[b]
-            slope = 2.0 * vol_ref[s] + bump_ref[b]
-            weighted = jnp.sum(sums_ref[pl.ds(s, 1), :], axis=1, keepdims=True)
-            total = jnp.where(lane == b, slope * weighted, total)
-        vega_ref[...] = total
+            s, _, change = picks[b]
+            held[b // SUB, here, b % SUB, :] = base + change * rows_ref[s + 1, here, :]
+        copy = pltpu.make_async_copy(held.at[:, here], out_ref.at[:, here], sem.at[i])
+        copy.start()
+        copies.append(copy)
+    lane = lax.broadcasted_iota(jnp.int32, (1, curves), 1)
+    total = jnp.zeros((1, curves), jnp.float32)
+    for b in range(curves):
+        s, slope, _ = picks[b]
+        weighted = jnp.sum(sums_ref[pl.ds(s, 1), :], axis=1, keepdims=True)
+        total = jnp.where(lane == b, slope * weighted, total)
+    vega_ref[...] = total
+    for copy in copies:
+        copy.wait()
 
 
 def on_device(n, nx, ny, payoff, positions, tables, offsets, vol_curve, bucket, bump_size):
@@ -343,8 +355,8 @@
     moved, sums = pl.pallas_call(
         functools.partial(sweep_kernel, (n, nx, ny, steps, per, block_len, chunks)),
         out_shape=(
-            jax.ShapeDtypeStruct((steps + 1, rows, LANES), jnp.float32),
-            jax.ShapeDtypeStruct((steps, LANES), jnp.float32),
+            pltpu.VMEM((steps + 1, rows, LANES), jnp.float32),
+            pltpu.VMEM((steps, LANES), jnp.float32),
         ),
         in_specs=[smem, vmem, vmem, vmem, pl.BlockSpec(memory_space=pl.ANY)],
         out_specs=(vmem, vmem),
@@ -368,37 +380,40 @@
             dma((n,)),
             dma((n,)),
         ],
-        compiler_params=pltpu.CompilerParams(has_side_effects=True, collective_id=0),
+        compiler_params=pltpu.CompilerParams(
+            has_side_effects=True, collective_id=0, vmem_limit_bytes=VMEM_LIMIT
+        ),
         name="sweep",
     )(
-        vol_curve,
-        payoff.reshape(rows, LANES),
-        positions.reshape(rows, LANES),
-        offsets,
-        tiles,
+        *[
+            pltpu.with_memory_space_constraint(x, pltpu.HBM)
+            for x in (
+                vol_curve,
+                payoff.reshape(rows, LANES),
+                positions.reshape(rows, LANES),
+                offsets,
+                tiles,
+            )
+        ]
     )
-    grid = max(1, n // 2)
     groups = curves // SUB
+    parts = max(1, rows // (4 * SUB))
     bumped, vega = pl.pallas_call(
         spread_kernel,
-        grid=(grid,),
         out_shape=(
             jax.ShapeDtypeStruct((groups, rows, SUB, LANES), jnp.float32),
             jax.ShapeDtypeStruct((1, curves), jnp.float32),
         ),
-        in_specs=[
-            smem,
-            smem,
-            smem,
-            pl.BlockSpec((steps + 1, rows // grid, LANES), lambda i: (0, i, 0)),
-            pl.BlockSpec((steps, LANES), lambda i: (0, 0)),
-        ],
-        out_specs=(
-            pl.BlockSpec((groups, rows // grid, SUB, LANES), lambda i: (0, i, 0, 0)),
-            pl.BlockSpec((1, curves), lambda i: (0, 0)),
-        ),
+        in_specs=[smem, smem, smem, vmem, vmem],
+        out_specs=(pl.BlockSpec(memory_space=pl.ANY), vmem),
+        scratch_shapes=[pltpu.VMEM((groups, rows, SUB, LANES), jnp.float32), dma((parts,))],
+        compiler_params=pltpu.CompilerParams(vmem_limit_bytes=VMEM_LIMIT),
         name="spread",
-    )(vol_curve, bucket, bump_size, moved, sums)
+    )(
+        *[pltpu.with_memory_space_constraint(x, pltpu.HBM) for x in (vol_curve, bucket, bump_size)],
+        moved,
+        sums,
+    )
     bumped = bumped.transpose(0, 2, 1, 3).reshape(curves, nodes)
     return bumped, vega.reshape(curves)
 

time: 37.8 us -> 36.6 us (0.968)
  Pallas kernels: 36.5 us -> 35.2 us
    pallas_call x1, Pallas kernels: 33 us -> 32 us  [on_device(): pl.pallas_call(functools.partial(sweep_kernel, (n, nx, ny, steps, per, bl...]
where the time goes in v1:
time: 36.6 us; the launch traced here: 35.8 us
  Pallas kernels  35.2 us (96%)
  between operations  0.64 us (2%)
    pallas_call x1, Pallas kernels, on_device(): pl.pallas_call(functools.partial(sweep_kernel, (n, nx, ny, steps, per, bl...  32 us
    pallas_call x1, Pallas kernels, on_device(): pl.pallas_call(spread_kernel, out_shape=(jax.ShapeDtypeStruct((groups, ro...  3.24 us

profile of v1, /device:TPU:5, one launch (start us, length us, event | category | flops | bytes accessed | tf_op | source)
XLA Modules:
  0.0 35.8 jit_solution(10622189631673668063)
XLA Ops:
  0.6 32.0 %sweep.1 = (f32[9,256,128]{2,1,0:T(8,128)S(1)}, f32[8,128]{1,0:T(8,128)S(1)}) custom-call(f32[8]{0:T(128)} %vol_ref.3, f32[256,128]{1,0:T(8,128)} %bitcast.12, f32[256,128]{1,0:T(8,128)} %bitcast.13, s32[8,128]{1,0:T(8,128)} %offsets_ref.1, f32[5,256,2,128]{3,2,1,0:T(2,128)} %bitcast.11), custom_call_target="tpu_custom_call" | custom-call | tf_op jit(solution)/shard_map/sweep/pallas_call | solution.py:355
  32.6 3.2 %spread.1 = (f32[2,256,8,128]{3,2,1,0:T(8,128)}, f32[1,16]{1,0:T(1,128)}) custom-call(f32[8]{0:T(128)} %vol_ref.3, s32[16]{0:T(128)} %bucket_ref.1, f32[16]{0:T(128)} %bump_ref.1, f32[9,256,128]{2,1,0:T(8,128)S(1)} %get-tuple-element.6.rows_ref, f32[8,128]{1,0:T(8,128)S(1)} %get-tuple-element.7.sums_ref), custom_call_target="tpu_custom_call" | custom-call | tf_op jit(solution)/shard_map/spread/pallas_call | solution.py:401

commit v2 on v1

v2 whole, which is shorter than its diff:
```python
import functools

import jax
import jax.numpy as jnp
from jax import lax
from jax.experimental import pallas as pl
from jax.experimental.pallas import tpu as pltpu
from jax.sharding import PartitionSpec as P

LANES = 128
SUB = 8
VMEM_LIMIT = 24 * 1024 * 1024
MESH = pl.DeviceIdType.MESH


def sweep_kernel(
    dims,
    vol_ref,
    payoff_ref,
    positions_ref,
    offsets_ref,
    tables_ref,
    rows_ref,
    sums_ref,
    tab,
    pay,
    pos,
    offs,
    coef,
    state,
    mid,
    part,
    tot,
    loc_sem,
    tab_send,
    tab_recv,
    halo_send,
    halo_recv,
    mid_send,
    mid_recv,
    far_send,
    far_recv,
    near_send,
    near_recv,
    ring_send,
    ring_recv,
    tot_send,
    tot_recv,
):
    n, nx, ny, steps, per, block_len, bounds = dims
    ring_size = nx * ny
    rows = payoff_ref.shape[0]
    blocks = offsets_ref.shape[1]
    group = n // 2
    half = steps // 2
    share = rows // group
    chunks = len(bounds) - 1
    me = lax.axis_index("bump")
    ring = lax.axis_index("nx") * ny + lax.axis_index("ny")
    side = me // group
    core = lax.rem(me, group)
    upper = side == 1
    lower = side == 0
    first = core == 0

    def at(r, q):
        return {"bump": q, "nx": r // ny, "ny": lax.rem(r, ny)}

    right = lax.rem(ring + 1, ring_size)
    left = lax.rem(ring + ring_size - 1, ring_size)
    sibling = at(ring, side * group + (1 - core))
    across = at(ring, (1 - side) * group + core)
    diagonal = at(ring, (1 - side) * group + (1 - core))
    outer = at(jnp.where(first, right, left), me)

    def start_of(c, a, b):
        return pl.multiple_of(SUB + jnp.where(c == 0, share - b, a), SUB)

    def local(a, b):
        return pl.ds(start_of(core, a, b), b - a)

    def wide_at(c, a, b):
        return pl.ds(pl.multiple_of(start_of(c, a, b) + c * share, SUB), b - a)

    def owned_at(c, a, b):
        return pl.ds(pl.multiple_of(start_of(c, a, b) + c * share - SUB, SUB), b - a)

    def table_at(c, a, b):
        begin = (start_of(c, a, b) + c * share) * per
        return pl.ds(pl.multiple_of(begin, SUB * per), (b - a) * per)

    whole = slice(SUB * per, (SUB + rows) * per)
    loads = [
        pltpu.make_async_copy(tables_ref, tab.at[core, :, whole], loc_sem.at[0]),
        pltpu.make_async_copy(payoff_ref, pay.at[SUB : SUB + rows], loc_sem.at[1]),
        pltpu.make_async_copy(positions_ref, pos, loc_sem.at[2]),
        pltpu.make_async_copy(offsets_ref, offs.at[0], loc_sem.at[3]),
    ]
    for copy in loads:
        copy.start()

    barrier = pltpu.get_barrier_semaphore()
    peers = [at(ring, lax.rem(me + i, n)) for i in range(1, n)]
    peers += [at(lax.rem(ring + i, ring_size), me) for i in range(1, ring_size)]
    for peer in peers:
        pl.semaphore_signal(barrier, inc=1, device_id=peer, device_id_type=MESH)
    for copy in loads:
        copy.wait()
    pl.semaphore_wait(barrier, len(peers))

    def remote(src, dst, send, recv, to):
        return pltpu.make_async_remote_copy(
            src_ref=src, dst_ref=dst, send_sem=send, recv_sem=recv, device_id=to, device_id_type=MESH
        )

    def fresh(j):
        lo = -SUB if j == 0 else min(bounds[j] + 2 * SUB, share)
        return lo, min(bounds[j + 1] + 2 * SUB, share)

    table_copies = []
    pieces = [fresh(j) for j in range(chunks)]
    for j, (lo, hi) in enumerate(pieces):
        there = tab.at[core, :, table_at(1 - core, lo, hi)]
        table_copies.append(remote(there, there, tab_send.at[j], tab_recv.at[j], sibling))
    there = tab.at[core, :, table_at(1 - core, share - SUB, share)]
    edge = pl.multiple_of(jnp.where(first, SUB, rows) * per, SUB * per)
    there = tab.at[core, :, pl.ds(edge, SUB * per)]
    table_copies.append(remote(there, there, tab_send.at[chunks], tab_recv.at[chunks], sibling))
    order = [0, chunks] + list(range(1, chunks))
    for j in order:
        table_copies[j].start()

    def arrived(j):
        lo, hi = pieces[j]
        here = tab.at[1 - core, :, table_at(core, lo, hi)]
        return remote(here, here, tab_send.at[j], tab_recv.at[j], sibling)

    out_from = pl.multiple_of(jnp.where(first, rows, SUB), SUB)
    out_to = pl.multiple_of(jnp.where(first, 0, rows + SUB), SUB)
    out_tab = pl.ds(pl.multiple_of(out_from * per, SUB * per), SUB * per)
    in_tab = pl.ds(pl.multiple_of(out_to * per, SUB * per), SUB * per)
    halo_copies = [
        remote(
            pay.at[pl.ds(out_from, SUB)], pay.at[pl.ds(out_to, SUB)],
            halo_send.at[0], halo_recv.at[0], outer,
        ),
        remote(offs.at[0], offs.at[1], halo_send.at[1], halo_recv.at[1], outer),
        remote(tab.at[:, :, out_tab], tab.at[:, :, in_tab], halo_send.at[2], halo_recv.at[2], outer),
    ]
    halo_copies[0].start()
    halo_copies[1].start()

    def send_tables_out():
        mine = remote(
            tab.at[1 - core, :, out_tab], tab.at[1 - core, :, out_tab],
            tab_send.at[chunks], tab_recv.at[chunks], sibling,
        )
        mine.wait_recv()
        halo_copies[2].start()

    def prepare(a, b, source):
        count = b - a
        begin = start_of(core, a, b)
        row = lax.broadcasted_iota(jnp.int32, (count, blocks), 0) + (begin - SUB + core * share + rows)
        hit = lax.broadcasted_iota(jnp.int32, (count, blocks), 1) == lax.rem(row, rows) * LANES // block_len
        here = pl.ds(begin, count)
        for t in range(half):
            step = side * half + t
            slot, at_step = t // per, t % per
            line = offs[source, pl.ds(step, 1), :].astype(jnp.float32)
            branch = jnp.sum(jnp.where(hit, line, 0.0), axis=1, keepdims=True)
            branch = jnp.broadcast_to(branch, (count, LANES))
            low = branch < -0.5
            high = branch > 0.5

            def entry(k):
                first_row = (begin + core * share) * per + at_step
                return tab[slot, k, pl.ds(first_row, count, stride=per), :]

            w = vol_ref[step] * vol_ref[step]
            discount = entry(0)
            slope_up = discount * entry(2)
            slope_down = discount * entry(4)
            up = discount * entry(1) + w * slope_up
            down = discount * entry(3) + w * slope_down
            middle = discount - up - down
            slope_mid = -slope_up - slope_down

            def put(k, above, level, below):
                zero = jnp.zeros_like(above)
                coef[t, k, here, :] = jnp.where(high, above, zero)
                coef[t, k + 1, here, :] = jnp.where(high, level, jnp.where(low, zero, above))
                coef[t, k + 2, here, :] = jnp.where(high, below, jnp.where(low, above, level))
                coef[t, k + 3, here, :] = jnp.where(high, zero, jnp.where(low, level, below))
                coef[t, k + 4, here, :] = jnp.where(low, below, zero)

            put(0, up, middle, down)
            put(5, slope_up, slope_mid, slope_down)

    def advance(a, b, top):
        count = b - a
        here = local(a, b)
        lane = lax.broadcasted_iota(jnp.int32, (count, LANES), 1)
        for t in reversed(range(half)):
            s = top + t
            c = [coef[t, k, here, :] for k in range(5)]
            for g in [0] + list(range(s + 2, steps + 1)):
                x = state[g, 0:count, :]
                after = pltpu.roll(x, count - 1, 0)
                before = pltpu.roll(x, 1, 0)
                f1 = pltpu.roll(jnp.where(lane < 1, after, x), LANES - 1, 1)
                f2 = pltpu.roll(jnp.where(lane < 2, after, x), LANES - 2, 1)
                b1 = pltpu.roll(jnp.where(lane >= LANES - 1, before, x), 1, 1)
                b2 = pltpu.roll(jnp.where(lane >= LANES - 2, before, x), 2, 1)
                state[g, 0:count, :] = c[0] * f2 + c[1] * f1 + c[2] * x + c[3] * b1 + c[4] * b2
                if g == 0:
                    e = [coef[t, 5 + k, here, :] for k in range(5)]
                    state[s + 1, 0:count, :] = e[0] * f2 + e[1] * f1 + e[2] * x + e[3] * b1 + e[4] * b2

    passed = [0] + list(range(half + 1, steps + 1))

    def mid_piece(j):
        return (-SUB if j == 0 else bounds[j] + SUB), bounds[j + 1] + SUB

    def mid_copy(j):
        lo, hi = mid_piece(j)
        here = mid.at[:, local(lo, hi)]
        return remote(here, here, mid_send.at[j], mid_recv.at[j], across)

    def result_at(c, j):
        return rows_ref.at[:, owned_at(c, bounds[j], bounds[j + 1])]

    def far_copy(j):
        here = result_at(core, j)
        return remote(here, here, far_send.at[j], far_recv.at[j], across)

    def near_copy(j):
        here = result_at(core, j)
        return remote(here, here, near_send.at[j], near_recv.at[j], sibling)

    def near_landed(j):
        here = result_at(1 - core, j)
        return remote(here, here, near_send.at[j], near_recv.at[j], sibling)

    @pl.when(upper)
    def _():
        for j in range(chunks):
            lo, hi = mid_piece(j)
            begin, end = max(lo - SUB, -SUB), min(hi + SUB, share + SUB)
            arrived(j).wait_recv()
            if j == 0:
                prepare(*pieces[0], 0)
                send_tables_out()
            elif pieces[j][0] < pieces[j][1]:
                prepare(*pieces[j], 0)
            if j == chunks - 1:
                for copy in halo_copies:
                    copy.wait_recv()
                prepare(share, share + SUB, 1)
            count = end - begin
            state[0, 0:count, :] = pay[wide_at(core, begin, end), :]
            advance(begin, end, half)
            shift = pl.multiple_of(jnp.where(first, end - hi, lo - begin), SUB)
            for i, g in enumerate(passed):
                mid[i, local(lo, hi), :] = state[g, pl.ds(shift, hi - lo), :]
            mid_copy(j).start()
        for j in range(chunks):
            far_copy(j).wait_recv()
            near_copy(j).start()
        for c in range(group):
            total = tot.at[c]
            remote(total, total, tot_send.at[c], tot_recv.at[c], across).wait_recv()
        for j in range(chunks):
            mid_copy(j).wait_send()

    @pl.when(lower)
    def _():
        for j in range(chunks):
            arrived(j).wait_recv()
            if j == 0:
                send_tables_out()
            if pieces[j][0] < pieces[j][1]:
                prepare(*pieces[j], 0)
        for j in range(chunks):
            lo, hi = bounds[j], bounds[j + 1]
            begin, end = lo - SUB, hi + SUB
            if j == chunks - 1:
                for copy in halo_copies:
                    copy.wait_recv()
                prepare(share, share + SUB, 1)
            mid_copy(j).wait_recv()
            count = end - begin
            for i, g in enumerate(passed):
                state[g, 0:count, :] = mid[i, local(begin, end), :]
            advance(begin, end, 0)
            here = owned_at(core, lo, hi)
            weights = pos[here, :]
            for g in range(steps + 1):
                center = state[g, SUB : SUB + hi - lo, :]
                rows_ref[g, here, :] = center
                if g:
                    weighted = jnp.sum(weights * center, axis=0, keepdims=True)
                    if j:
                        weighted = weighted + part[ring, g - 1 : g, :]
                    part[ring, g - 1 : g, :] = weighted
            far_copy(j).start()
            near_copy(j).start()
        ring_copies = []
        for i in range(1, ring_size):
            mine = part.at[ring]
            to = at(lax.rem(ring + i, ring_size), me)
            ring_copies.append(remote(mine, mine, ring_send.at[i], ring_recv.at[i], to))
        for copy in ring_copies:
            copy.start()
        for i in range(1, ring_size):
            other = part.at[lax.rem(ring + ring_size - i, ring_size)]
            remote(other, other, ring_send.at[i], ring_recv.at[i], sibling).wait_recv()
        tot[core] = jnp.sum(part[...], axis=0)
        total = tot.at[core]
        tot_copies = [
            remote(total, total, tot_send.at[i], tot_recv.at[core], to)
            for i, to in enumerate((sibling, across, diagonal))
        ]
        for copy in tot_copies:
            copy.start()
        other = tot.at[1 - core]
        remote(other, other, tot_send.at[0], tot_recv.at[1 - core], sibling).wait_recv()
        for copy in ring_copies + tot_copies:
            copy.wait_send()
        for j in range(chunks):
            far_copy(j).wait_send()

    sums_ref[...] = jnp.sum(tot[...], axis=0)
    for j in range(chunks):
        near_landed(j).wait_recv()
        near_copy(j).wait_send()
    for copy in table_copies + halo_copies:
        copy.wait_send()


def spread_kernel(vol_ref, bucket_ref, bump_ref, rows_ref, sums_ref, out_ref, vega_ref, held, sem):
    curves = bucket_ref.shape[0]
    groups = curves // SUB
    rows = rows_ref.shape[1]
    parts = sem.shape[0]
    span = rows // parts
    picks = []
    for b in range(curves):
        s = bucket_ref[b]
        slope = 2.0 * vol_ref[s] + bump_ref[b]
        picks.append((s, slope, bump_ref[b] * slope))
    copies = []
    for i in range(parts):
        here = slice(i * span, (i + 1) * span)
        base = rows_ref[0, here, :]
        for b in range(curves):
            s, _, change = picks[b]
            line = (b // SUB * rows + i * span) * SUB + b % SUB
            held[pl.ds(line, span, stride=SUB), :] = base + change * rows_ref[s + 1, here, :]
        for g in range(groups):
            place = slice((g * rows + i * span) * SUB, (g * rows + (i + 1) * span) * SUB)
            copy = pltpu.make_async_copy(held.at[place], out_ref.at[place], sem.at[i, g])
            copy.start()
            copies.append(copy)
    lane = lax.broadcasted_iota(jnp.int32, (1, curves), 1)
    total = jnp.zeros((1, curves), jnp.float32)
    for b in range(curves):
        s, slope, _ = picks[b]
        weighted = jnp.sum(sums_ref[pl.ds(s, 1), :], axis=1, keepdims=True)
        total = jnp.where(lane == b, slope * weighted, total)
    vega_ref[...] = total
    for copy in copies:
        copy.wait()


def on_device(n, nx, ny, payoff, positions, tables, offsets, vol_curve, bucket, bump_size):
    steps = vol_curve.shape[0]
    per, comps, nodes = tables.shape
    curves = bucket.shape[0]
    rows = nodes // LANES
    block_len = nodes // offsets.shape[1]
    group = n // 2
    share = rows // group
    half = steps // 2
    ring = nx * ny
    bounds = [share * k // (8 * SUB) * SUB for k in (0, 1, 3, 5, 8)]
    chunks = len(bounds) - 1
    widest = max(b - a for a, b in zip(bounds, bounds[1:])) + 3 * SUB
    tiles = tables.transpose(1, 0, 2).reshape(comps, per, rows, LANES).transpose(0, 2, 1, 3)
    tiles = tiles.reshape(comps, rows * per, LANES)
    dma = pltpu.SemaphoreType.DMA
    vmem = pl.BlockSpec(memory_space=pltpu.VMEM)
    smem = pl.BlockSpec(memory_space=pltpu.SMEM)
    hbm = pl.BlockSpec(memory_space=pltpu.HBM)

    def keep(x):
        return pltpu.with_memory_space_constraint(x, pltpu.HBM)

    moved, sums = pl.pallas_call(
        functools.partial(sweep_kernel, (n, nx, ny, steps, per, block_len, bounds)),
        out_shape=(
            pltpu.VMEM((steps + 1, rows, LANES), jnp.float32),
            pltpu.VMEM((steps, LANES), jnp.float32),
        ),
        in_specs=[smem, hbm, hbm, hbm, hbm],
        out_specs=(vmem, vmem),
        scratch_shapes=[
            pltpu.VMEM((group, comps, (rows + 2 * SUB) * per, LANES), jnp.float32),
            pltpu.VMEM((rows + 2 * SUB, LANES), jnp.float32),
            pltpu.VMEM((rows, LANES), jnp.float32),
            pltpu.VMEM((2,) + offsets.shape, jnp.int32),
            pltpu.VMEM((half, 10, share + 2 * SUB, LANES), jnp.float32),
            pltpu.VMEM((steps + 1, widest, LANES), jnp.float32),
            pltpu.VMEM((half + 1, share + 2 * SUB, LANES), jnp.float32),
            pltpu.VMEM((ring, steps, LANES), jnp.float32),
            pltpu.VMEM((group, steps, LANES), jnp.float32),
            dma((4,)),
            dma((chunks + 1,)),
            dma((chunks + 1,)),
            dma((3,)),
            dma((3,)),
            dma((chunks,)),
            dma((chunks,)),
            dma((chunks,)),
            dma((chunks,)),
            dma((chunks,)),
            dma((chunks,)),
            dma((ring,)),
            dma((ring,)),
            dma((3,)),
            dma((group,)),
        ],
        compiler_params=pltpu.CompilerParams(
            has_side_effects=True, collective_id=0, vmem_limit_bytes=VMEM_LIMIT
        ),
        name="sweep",
    )(
        keep(vol_curve),
        keep(payoff.reshape(rows, LANES)),
        keep(positions.reshape(rows, LANES)),
        keep(offsets),
        keep(tiles),
    )
    groups = curves // SUB
    parts = max(1, rows // (4 * SUB))
    bumped, vega = pl.pallas_call(
        spread_kernel,
        out_shape=(
            jax.ShapeDtypeStruct((groups * rows * SUB, LANES), jnp.float32),
            jax.ShapeDtypeStruct((1, curves), jnp.float32),
        ),
        in_specs=[smem, smem, smem, vmem, vmem],
        out_specs=(pl.BlockSpec(memory_space=pl.ANY), vmem),
        scratch_shapes=[pltpu.VMEM((groups * rows * SUB, LANES), jnp.float32), dma((parts, groups))],
        compiler_params=pltpu.CompilerParams(vmem_limit_bytes=VMEM_LIMIT),
        name="spread",
    )(keep(vol_curve), keep(bucket), keep(bump_size), moved, sums)
    bumped = bumped.reshape(groups, rows, SUB, LANES).transpose(0, 2, 1, 3).reshape(curves, nodes)
    return bumped, vega.reshape(curves)


def solution(mesh):
    shape = dict(mesh.shape)
    in_specs = (
        P(("nx", "ny")),
        P(("nx", "ny")),
        P("bump", None, ("nx", "ny")),
        P(None, ("nx", "ny")),
        P(),
        P("bump"),
        P("bump"),
    )
    out_specs = (P("bump", ("nx", "ny")), P("bump"))
    body = functools.partial(on_device, shape["bump"], shape["nx"], shape["ny"])
    return jax.shard_map(body, mesh=mesh, in_specs=in_specs, out_specs=out_specs, check_vma=False)
```

time: 36.6 us -> 32.3 us (0.88); the launches traced: 35.8 us -> 32.1 us
  Pallas kernels: 35.2 us -> 31.5 us
    pallas_call x1, Pallas kernels: 32 us -> 28.8 us  [on_device(): pl.pallas_call(functools.partial(sweep_kernel, (n, nx, ny, steps, per, bl...]
    pallas_call x1, Pallas kernels: 3.24 us -> 2.7 us  [on_device(): pl.pallas_call(spread_kernel, out_shape=(jax.ShapeDtypeStruct((groups * r...]
where the time goes in v2:
time: 32.3 us; the launch traced here: 32.1 us
  Pallas kernels  31.5 us (98%)
  between operations  0.64 us (2%)
    pallas_call x1, Pallas kernels, on_device(): pl.pallas_call(functools.partial(sweep_kernel, (n, nx, ny, steps, per, bl...  28.8 us
    pallas_call x1, Pallas kernels, on_device(): pl.pallas_call(spread_kernel, out_shape=(jax.ShapeDtypeStruct((groups * r...  2.7 us

profile of v2, /device:TPU:5, one launch (start us, length us, event | category | flops | bytes accessed | tf_op | source)
XLA Modules:
  0.0 32.1 jit_solution(3766013272068239168)
XLA Ops:
  0.6 28.8 %sweep.1 = (f32[9,256,128]{2,1,0:T(8,128)S(1)}, f32[8,128]{1,0:T(8,128)S(1)}) custom-call(f32[8]{0:T(128)} %vol_ref.3, f32[256,128]{1,0:T(8,128)} %bitcast.16, f32[256,128]{1,0:T(8,128)} %bitcast.17, s32[8,128]{1,0:T(8,128)} %offsets_ref.1, f32[5,512,128]{2,1,0:T(8,128)} %bitcast.15), custom_call_target="tpu_custom_call" | custom-call | tf_op jit(solution)/shard_map/sweep/pallas_call | solution.py:399
  29.4 2.7 %spread.1 = (f32[4096,128]{1,0:T(8,128)}, f32[1,16]{1,0:T(1,128)}) custom-call(f32[8]{0:T(128)} %vol_ref.3, s32[16]{0:T(128)} %bucket_ref.1, f32[16]{0:T(128)} %bump_ref.1, f32[9,256,128]{2,1,0:T(8,128)S(1)} %get-tuple-element.6.rows_ref, f32[8,128]{1,0:T(8,128)S(1)} %get-tuple-element.7.sums_ref), custom_call_target="tpu_custom_call" | custom-call | tf_op jit(solution)/shard_map/spread/pallas_call | solution.py:446

commit v3 on v2

--- a/solution.py
+++ b/solution.py
@@ -31,6 +31,7 @@
     mid,
     part,
     tot,
+    hello,
     loc_sem,
     tab_send,
     tab_recv,
@@ -100,13 +101,43 @@
         copy.start()
 
     barrier = pltpu.get_barrier_semaphore()
-    peers = [at(ring, lax.rem(me + i, n)) for i in range(1, n)]
-    peers += [at(lax.rem(ring + i, ring_size), me) for i in range(1, ring_size)]
-    for peer in peers:
-        pl.semaphore_signal(barrier, inc=1, device_id=peer, device_id_type=MESH)
-    for copy in loads:
-        copy.wait()
-    pl.semaphore_wait(barrier, len(peers))
+
+    def greet(sem, to):
+        pl.semaphore_signal(sem, inc=1, device_id=to, device_id_type=MESH)
+
+    keeper = jnp.logical_and(lower, first)
+    link = jnp.logical_and(upper, first)
+    rest = jnp.logical_not(first)
+
+    @pl.when(link)
+    def _():
+        greet(barrier, sibling)
+        greet(barrier, at(left, 0))
+
+    @pl.when(jnp.logical_and(upper, rest))
+    def _():
+        greet(barrier, at(right, 0))
+
+    @pl.when(lower)
+    def _():
+        greet(barrier, at(ring, group))
+        for i in range(1, ring_size):
+            greet(barrier, at(lax.rem(ring + i, ring_size), 0))
+
+    @pl.when(keeper)
+    def _():
+        greet(barrier, sibling)
+
+    @pl.when(rest)
+    def _():
+        pl.semaphore_wait(barrier, 1)
+        greet(hello.at[0], sibling)
+
+    @pl.when(first)
+    def _():
+        pl.semaphore_wait(hello.at[0], 1)
+
+    loads[0].wait()
 
     def remote(src, dst, send, recv, to):
         return pltpu.make_async_remote_copy(
@@ -122,11 +153,10 @@
     for j, (lo, hi) in enumerate(pieces):
         there = tab.at[core, :, table_at(1 - core, lo, hi)]
         table_copies.append(remote(there, there, tab_send.at[j], tab_recv.at[j], sibling))
-    there = tab.at[core, :, table_at(1 - core, share - SUB, share)]
     edge = pl.multiple_of(jnp.where(first, SUB, rows) * per, SUB * per)
     there = tab.at[core, :, pl.ds(edge, SUB * per)]
     table_copies.append(remote(there, there, tab_send.at[chunks], tab_recv.at[chunks], sibling))
-    order = [0, chunks] + list(range(1, chunks))
+    order = [j for j, (lo, hi) in enumerate(pieces) if lo < hi] + [chunks]
     for j in order:
         table_copies[j].start()
 
@@ -147,16 +177,12 @@
         remote(offs.at[0], offs.at[1], halo_send.at[1], halo_recv.at[1], outer),
         remote(tab.at[:, :, out_tab], tab.at[:, :, in_tab], halo_send.at[2], halo_recv.at[2], outer),
     ]
-    halo_copies[0].start()
-    halo_copies[1].start()
-
-    def send_tables_out():
-        mine = remote(
-            tab.at[1 - core, :, out_tab], tab.at[1 - core, :, out_tab],
-            tab_send.at[chunks], tab_recv.at[chunks], sibling,
-        )
-        mine.wait_recv()
-        halo_copies[2].start()
+    landed = remote(
+        tab.at[1 - core, :, out_tab], tab.at[1 - core, :, out_tab],
+        tab_send.at[chunks], tab_recv.at[chunks], sibling,
+    )
+
+    loads[3].wait()
 
     def prepare(a, b, source):
         count = b - a
@@ -244,16 +270,18 @@
 
     @pl.when(upper)
     def _():
+        loads[1].wait()
         for j in range(chunks):
             lo, hi = mid_piece(j)
             begin, end = max(lo - SUB, -SUB), min(hi + SUB, share + SUB)
-            arrived(j).wait_recv()
-            if j == 0:
-                prepare(*pieces[0], 0)
-                send_tables_out()
-            elif pieces[j][0] < pieces[j][1]:
+            if pieces[j][0] < pieces[j][1]:
+                arrived(j).wait_recv()
                 prepare(*pieces[j], 0)
             if j == chunks - 1:
+                landed.wait_recv()
+                pl.semaphore_wait(hello.at[2], 1)
+                for copy in halo_copies:
+                    copy.start()
                 for copy in halo_copies:
                     copy.wait_recv()
                 prepare(share, share + SUB, 1)
@@ -263,7 +291,20 @@
             shift = pl.multiple_of(jnp.where(first, end - hi, lo - begin), SUB)
             for i, g in enumerate(passed):
                 mid[i, local(lo, hi), :] = state[g, pl.ds(shift, hi - lo), :]
+            if j == 0:
+
+                @pl.when(first)
+                def _():
+                    pl.semaphore_wait(barrier, 2)
+                    greet(hello.at[1], sibling)
+
+                @pl.when(rest)
+                def _():
+                    pl.semaphore_wait(hello.at[1], 1)
+
             mid_copy(j).start()
+        for copy in halo_copies:
+            copy.wait_send()
         for j in range(chunks):
             far_copy(j).wait_recv()
             near_copy(j).start()
@@ -275,17 +316,32 @@
 
     @pl.when(lower)
     def _():
+        loads[2].wait()
+        landed.wait_recv()
         for j in range(chunks):
-            arrived(j).wait_recv()
-            if j == 0:
-                send_tables_out()
             if pieces[j][0] < pieces[j][1]:
+                arrived(j).wait_recv()
                 prepare(*pieces[j], 0)
         for j in range(chunks):
             lo, hi = bounds[j], bounds[j + 1]
             begin, end = lo - SUB, hi + SUB
+            if j == 2:
+
+                @pl.when(first)
+                def _():
+                    pl.semaphore_wait(barrier, 2 * ring_size)
+                    greet(hello.at[2], sibling)
+                    greet(hello.at[2], across)
+                    greet(hello.at[2], diagonal)
+
+                @pl.when(rest)
+                def _():
+                    pl.semaphore_wait(hello.at[2], 1)
+
+                for copy in halo_copies[1:]:
+                    copy.start()
             if j == chunks - 1:
-                for copy in halo_copies:
+                for copy in halo_copies[1:]:
                     copy.wait_recv()
                 prepare(share, share + SUB, 1)
             mid_copy(j).wait_recv()
@@ -325,7 +381,7 @@
             copy.start()
         other = tot.at[1 - core]
         remote(other, other, tot_send.at[0], tot_recv.at[1 - core], sibling).wait_recv()
-        for copy in ring_copies + tot_copies:
+        for copy in ring_copies + tot_copies + halo_copies[1:]:
             copy.wait_send()
         for j in range(chunks):
             far_copy(j).wait_send()
@@ -334,8 +390,16 @@
     for j in range(chunks):
         near_landed(j).wait_recv()
         near_copy(j).wait_send()
-    for copy in table_copies + halo_copies:
-        copy.wait_send()
+    for j in order:
+        table_copies[j].wait_send()
+
+    @pl.when(upper)
+    def _():
+        loads[2].wait()
+
+    @pl.when(lower)
+    def _():
+        loads[1].wait()
 
 
 def spread_kernel(vol_ref, bucket_ref, bump_ref, rows_ref, sums_ref, out_ref, vega_ref, held, sem):
@@ -383,7 +447,7 @@
     share = rows // group
     half = steps // 2
     ring = nx * ny
-    bounds = [share * k // (8 * SUB) * SUB for k in (0, 1, 3, 5, 8)]
+    bounds = [share * k // (16 * SUB) * SUB for k in (0, 2, 5, 9, 13, 16)]
     chunks = len(bounds) - 1
     widest = max(b - a for a, b in zip(bounds, bounds[1:])) + 3 * SUB
     tiles = tables.transpose(1, 0, 2).reshape(comps, per, rows, LANES).transpose(0, 2, 1, 3)
@@ -414,6 +478,7 @@
             pltpu.VMEM((half + 1, share + 2 * SUB, LANES), jnp.float32),
             pltpu.VMEM((ring, steps, LANES), jnp.float32),
             pltpu.VMEM((group, steps, LANES), jnp.float32),
+            pltpu.SemaphoreType.REGULAR((3,)),
             dma((4,)),
             dma((chunks + 1,)),
             dma((chunks + 1,)),

time: 32.3 us -> 32.1 us (level)
  Pallas kernels: 31.5 us -> 31.1 us
    pallas_call x1, Pallas kernels: 28.8 us -> 28.4 us  [on_device(): pl.pallas_call(functools.partial(sweep_kernel, (n, nx, ny, steps, per, bl...]
where the time goes in v3:
time: 32.1 us; the launch traced here: 31.7 us
  Pallas kernels  31.1 us (97%)
  between operations  0.64 us (2%)
    pallas_call x1, Pallas kernels, on_device(): pl.pallas_call(functools.partial(sweep_kernel, (n, nx, ny, steps, per, bl...  28.4 us
    pallas_call x1, Pallas kernels, on_device(): pl.pallas_call(spread_kernel, out_shape=(jax.ShapeDtypeStruct((groups * r...  2.7 us

profile of v3, /device:TPU:5, one launch (start us, length us, event | category | flops | bytes accessed | tf_op | source)
XLA Modules:
  0.0 31.7 jit_solution(13524731662435019553)
XLA Ops:
  0.6 28.4 %sweep.1 = (f32[9,256,128]{2,1,0:T(8,128)S(1)}, f32[8,128]{1,0:T(8,128)S(1)}) custom-call(f32[8]{0:T(128)} %vol_ref.3, f32[256,128]{1,0:T(8,128)} %bitcast.16, f32[256,128]{1,0:T(8,128)} %bitcast.17, s32[8,128]{1,0:T(8,128)} %offsets_ref.1, f32[5,512,128]{2,1,0:T(8,128)} %bitcast.15), custom_call_target="tpu_custom_call" | custom-call | tf_op jit(solution)/shard_map/sweep/pallas_call | solution.py:463
  29.0 2.7 %spread.1 = (f32[4096,128]{1,0:T(8,128)}, f32[1,16]{1,0:T(1,128)}) custom-call(f32[8]{0:T(128)} %vol_ref.3, s32[16]{0:T(128)} %bucket_ref.1, f32[16]{0:T(128)} %bump_ref.1, f32[9,256,128]{2,1,0:T(8,128)S(1)} %get-tuple-element.6.rows_ref, f32[8,128]{1,0:T(8,128)S(1)} %get-tuple-element.7.sums_ref), custom_call_target="tpu_custom_call" | custom-call | tf_op jit(solution)/shard_map/spread/pallas_call | solution.py:511

commit v4 on v3

--- a/solution.py
+++ b/solution.py
@@ -15,13 +15,18 @@
 
 def sweep_kernel(
     dims,
-    vol_ref,
+    curve_ref,
+    bucket_ref,
+    bump_ref,
     payoff_ref,
     positions_ref,
     offsets_ref,
     tables_ref,
     rows_ref,
     sums_ref,
+    vol_ref,
+    picks_ref,
+    sizes_ref,
     tab,
     pay,
     pos,
@@ -31,6 +36,8 @@
     mid,
     part,
     tot,
+    edge_out,
+    edge_in,
     hello,
     loc_sem,
     tab_send,
@@ -52,6 +59,7 @@
     ring_size = nx * ny
     rows = payoff_ref.shape[0]
     blocks = offsets_ref.shape[1]
+    comps = tables_ref.shape[0]
     group = n // 2
     half = steps // 2
     share = rows // group
@@ -96,9 +104,10 @@
         pltpu.make_async_copy(payoff_ref, pay.at[SUB : SUB + rows], loc_sem.at[1]),
         pltpu.make_async_copy(positions_ref, pos, loc_sem.at[2]),
         pltpu.make_async_copy(offsets_ref, offs.at[0], loc_sem.at[3]),
+        pltpu.make_async_copy(curve_ref, vol_ref, loc_sem.at[4]),
+        pltpu.make_async_copy(bucket_ref, picks_ref, loc_sem.at[5]),
+        pltpu.make_async_copy(bump_ref, sizes_ref, loc_sem.at[6]),
     ]
-    for copy in loads:
-        copy.start()
 
     barrier = pltpu.get_barrier_semaphore()
 
@@ -112,10 +121,12 @@
     @pl.when(link)
     def _():
         greet(barrier, sibling)
+        greet(barrier, at(ring, 0))
         greet(barrier, at(left, 0))
 
     @pl.when(jnp.logical_and(upper, rest))
     def _():
+        greet(barrier, at(ring, 0))
         greet(barrier, at(right, 0))
 
     @pl.when(lower)
@@ -127,6 +138,9 @@
     @pl.when(keeper)
     def _():
         greet(barrier, sibling)
+
+    for copy in loads:
+        copy.start()
 
     @pl.when(rest)
     def _():
@@ -152,10 +166,10 @@
     pieces = [fresh(j) for j in range(chunks)]
     for j, (lo, hi) in enumerate(pieces):
         there = tab.at[core, :, table_at(1 - core, lo, hi)]
-        table_copies.append(remote(there, there, tab_send.at[j], tab_recv.at[j], sibling))
+        table_copies.append(remote(there, there, tab_send, tab_recv.at[j], sibling))
     edge = pl.multiple_of(jnp.where(first, SUB, rows) * per, SUB * per)
     there = tab.at[core, :, pl.ds(edge, SUB * per)]
-    table_copies.append(remote(there, there, tab_send.at[chunks], tab_recv.at[chunks], sibling))
+    table_copies.append(remote(there, there, tab_send, tab_recv.at[chunks], sibling))
     order = [j for j, (lo, hi) in enumerate(pieces) if lo < hi] + [chunks]
     for j in order:
         table_copies[j].start()
@@ -163,26 +177,51 @@
     def arrived(j):
         lo, hi = pieces[j]
         here = tab.at[1 - core, :, table_at(core, lo, hi)]
-        return remote(here, here, tab_send.at[j], tab_recv.at[j], sibling)
+        return remote(here, here, tab_send, tab_recv.at[j], sibling)
 
     out_from = pl.multiple_of(jnp.where(first, rows, SUB), SUB)
     out_to = pl.multiple_of(jnp.where(first, 0, rows + SUB), SUB)
-    out_tab = pl.ds(pl.multiple_of(out_from * per, SUB * per), SUB * per)
-    in_tab = pl.ds(pl.multiple_of(out_to * per, SUB * per), SUB * per)
     halo_copies = [
         remote(
             pay.at[pl.ds(out_from, SUB)], pay.at[pl.ds(out_to, SUB)],
             halo_send.at[0], halo_recv.at[0], outer,
         ),
         remote(offs.at[0], offs.at[1], halo_send.at[1], halo_recv.at[1], outer),
-        remote(tab.at[:, :, out_tab], tab.at[:, :, in_tab], halo_send.at[2], halo_recv.at[2], outer),
+        remote(edge_out, edge_in, halo_send.at[2], halo_recv.at[2], outer),
     ]
-    landed = remote(
-        tab.at[1 - core, :, out_tab], tab.at[1 - core, :, out_tab],
-        tab_send.at[chunks], tab_recv.at[chunks], sibling,
-    )
+
+    lines = [(slot, k, (slot * comps + k) * per) for slot in range(group) for k in range(comps)]
+
+    def gather_edge():
+        taken = tab.at[1 - core, :, pl.ds(pl.multiple_of(out_from * per, SUB * per), SUB * per)]
+        remote(taken, taken, tab_send, tab_recv.at[chunks], sibling).wait_recv()
+
+        @pl.when(first)
+        def _():
+            for slot, k, line in lines:
+                at_row = (SUB + rows - 1) * per
+                edge_out[line : line + per, :] = tab[slot, k, at_row : at_row + per, :]
+
+        @pl.when(rest)
+        def _():
+            for slot, k, line in lines:
+                edge_out[line : line + per, :] = tab[slot, k, SUB * per : (SUB + 1) * per, :]
+
+    def place_edge():
+        @pl.when(first)
+        def _():
+            for slot, k, line in lines:
+                at_row = (SUB - 1) * per
+                tab[slot, k, at_row : at_row + per, :] = edge_in[line : line + per, :]
+
+        @pl.when(rest)
+        def _():
+            for slot, k, line in lines:
+                at_row = (SUB + rows) * per
+                tab[slot, k, at_row : at_row + per, :] = edge_in[line : line + per, :]
 
     loads[3].wait()
+    loads[4].wait()
 
     def prepare(a, b, source):
         count = b - a
@@ -251,22 +290,24 @@
     def mid_copy(j):
         lo, hi = mid_piece(j)
         here = mid.at[:, local(lo, hi)]
-        return remote(here, here, mid_send.at[j], mid_recv.at[j], across)
+        return remote(here, here, mid_send, mid_recv.at[j], across)
 
     def result_at(c, j):
         return rows_ref.at[:, owned_at(c, bounds[j], bounds[j + 1])]
 
     def far_copy(j):
         here = result_at(core, j)
-        return remote(here, here, far_send.at[j], far_recv.at[j], across)
+        return remote(here, here, far_send, far_recv.at[j], across)
 
     def near_copy(j):
         here = result_at(core, j)
-        return remote(here, here, near_send.at[j], near_recv.at[j], sibling)
-
-    def near_landed(j):
-        here = result_at(1 - core, j)
-        return remote(here, here, near_send.at[j], near_recv.at[j], sibling)
+        return remote(here, here, near_send, near_recv, sibling)
+
+    def all_of(ref, sem):
+        pltpu.make_async_copy(ref, ref, sem).wait()
+
+    mine = rows_ref.at[:, owned_at(core, 0, share)]
+    others = rows_ref.at[:, owned_at(1 - core, 0, share)]
 
     @pl.when(upper)
     def _():
@@ -278,12 +319,13 @@
                 arrived(j).wait_recv()
                 prepare(*pieces[j], 0)
             if j == chunks - 1:
-                landed.wait_recv()
+                gather_edge()
                 pl.semaphore_wait(hello.at[2], 1)
                 for copy in halo_copies:
                     copy.start()
                 for copy in halo_copies:
                     copy.wait_recv()
+                place_edge()
                 prepare(share, share + SUB, 1)
             count = end - begin
             state[0, 0:count, :] = pay[wide_at(core, begin, end), :]
@@ -308,16 +350,13 @@
         for j in range(chunks):
             far_copy(j).wait_recv()
             near_copy(j).start()
-        for c in range(group):
-            total = tot.at[c]
-            remote(total, total, tot_send.at[c], tot_recv.at[c], across).wait_recv()
-        for j in range(chunks):
-            mid_copy(j).wait_send()
+        all_of(tot, tot_recv)
+        all_of(mid, mid_send)
 
     @pl.when(lower)
     def _():
         loads[2].wait()
-        landed.wait_recv()
+        gather_edge()
         for j in range(chunks):
             if pieces[j][0] < pieces[j][1]:
                 arrived(j).wait_recv()
@@ -325,24 +364,28 @@
         for j in range(chunks):
             lo, hi = bounds[j], bounds[j + 1]
             begin, end = lo - SUB, hi + SUB
-            if j == 2:
+            if j == 1:
 
                 @pl.when(first)
                 def _():
-                    pl.semaphore_wait(barrier, 2 * ring_size)
+                    pl.semaphore_wait(barrier, 2 * ring_size + 2)
                     greet(hello.at[2], sibling)
                     greet(hello.at[2], across)
                     greet(hello.at[2], diagonal)
 
+            if j == 2:
+
                 @pl.when(rest)
                 def _():
                     pl.semaphore_wait(hello.at[2], 1)
 
+            if j == 2:
                 for copy in halo_copies[1:]:
                     copy.start()
             if j == chunks - 1:
                 for copy in halo_copies[1:]:
                     copy.wait_recv()
+                place_edge()
                 prepare(share, share + SUB, 1)
             mid_copy(j).wait_recv()
             count = end - begin
@@ -361,37 +404,27 @@
                     part[ring, g - 1 : g, :] = weighted
             far_copy(j).start()
             near_copy(j).start()
-        ring_copies = []
         for i in range(1, ring_size):
-            mine = part.at[ring]
-            to = at(lax.rem(ring + i, ring_size), me)
-            ring_copies.append(remote(mine, mine, ring_send.at[i], ring_recv.at[i], to))
-        for copy in ring_copies:
-            copy.start()
-        for i in range(1, ring_size):
-            other = part.at[lax.rem(ring + ring_size - i, ring_size)]
-            remote(other, other, ring_send.at[i], ring_recv.at[i], sibling).wait_recv()
+            own = part.at[ring]
+            remote(own, own, ring_send, ring_recv, at(lax.rem(ring + i, ring_size), me)).start()
+        all_of(part.at[1:ring_size], ring_recv)
         tot[core] = jnp.sum(part[...], axis=0)
         total = tot.at[core]
-        tot_copies = [
-            remote(total, total, tot_send.at[i], tot_recv.at[core], to)
-            for i, to in enumerate((sibling, across, diagonal))
-        ]
-        for copy in tot_copies:
-            copy.start()
-        other = tot.at[1 - core]
-        remote(other, other, tot_send.at[0], tot_recv.at[1 - core], sibling).wait_recv()
-        for copy in ring_copies + tot_copies + halo_copies[1:]:
+        for to in (sibling, across, diagonal):
+            remote(total, total, tot_send, tot_recv, to).start()
+        all_of(tot.at[1 - core], tot_recv)
+        all_of(part.at[1:ring_size], ring_send)
+        all_of(pay.at[0 : 3 * steps], tot_send)
+        for copy in halo_copies[1:]:
             copy.wait_send()
-        for j in range(chunks):
-            far_copy(j).wait_send()
+        all_of(mine, far_send)
 
     sums_ref[...] = jnp.sum(tot[...], axis=0)
-    for j in range(chunks):
-        near_landed(j).wait_recv()
-        near_copy(j).wait_send()
-    for j in order:
-        table_copies[j].wait_send()
+    all_of(others, near_recv)
+    all_of(mine, near_send)
+    all_of(tab.at[core, :, 0 : (share + 2 * SUB) * per], tab_send)
+    loads[5].wait()
+    loads[6].wait()
 
     @pl.when(upper)
     def _():
@@ -402,7 +435,9 @@
         loads[1].wait()
 
 
-def spread_kernel(vol_ref, bucket_ref, bump_ref, rows_ref, sums_ref, out_ref, vega_ref, held, sem):
+def spread_kernel(
+    vol_ref, bucket_ref, bump_ref, rows_ref, sums_ref, out_ref, vega_ref, held, small, sem, small_sem
+):
     curves = bucket_ref.shape[0]
     groups = curves // SUB
     rows = rows_ref.shape[1]
@@ -413,7 +448,15 @@
         s = bucket_ref[b]
         slope = 2.0 * vol_ref[s] + bump_ref[b]
         picks.append((s, slope, bump_ref[b] * slope))
-    copies = []
+    lane = lax.broadcasted_iota(jnp.int32, (1, curves), 1)
+    total = jnp.zeros((1, curves), jnp.float32)
+    for b in range(curves):
+        s, slope, _ = picks[b]
+        weighted = jnp.sum(sums_ref[pl.ds(s, 1), :], axis=1, keepdims=True)
+        total = jnp.where(lane == b, slope * weighted, total)
+    small[...] = total
+    copies = [pltpu.make_async_copy(small, vega_ref, small_sem)]
+    copies[0].start()
     for i in range(parts):
         here = slice(i * span, (i + 1) * span)
         base = rows_ref[0, here, :]
@@ -426,13 +469,6 @@
             copy = pltpu.make_async_copy(held.at[place], out_ref.at[place], sem.at[i, g])
             copy.start()
             copies.append(copy)
-    lane = lax.broadcasted_iota(jnp.int32, (1, curves), 1)
-    total = jnp.zeros((1, curves), jnp.float32)
-    for b in range(curves):
-        s, slope, _ = picks[b]
-        weighted = jnp.sum(sums_ref[pl.ds(s, 1), :], axis=1, keepdims=True)
-        total = jnp.where(lane == b, slope * weighted, total)
-    vega_ref[...] = total
     for copy in copies:
         copy.wait()
 
@@ -460,14 +496,17 @@
     def keep(x):
         return pltpu.with_memory_space_constraint(x, pltpu.HBM)
 
-    moved, sums = pl.pallas_call(
+    moved, sums, vol_on, bucket_on, bump_on = pl.pallas_call(
         functools.partial(sweep_kernel, (n, nx, ny, steps, per, block_len, bounds)),
         out_shape=(
             pltpu.VMEM((steps + 1, rows, LANES), jnp.float32),
             pltpu.VMEM((steps, LANES), jnp.float32),
+            pltpu.SMEM(vol_curve.shape, vol_curve.dtype),
+            pltpu.SMEM(bucket.shape, bucket.dtype),
+            pltpu.SMEM(bump_size.shape, bump_size.dtype),
         ),
-        in_specs=[smem, hbm, hbm, hbm, hbm],
-        out_specs=(vmem, vmem),
+        in_specs=[hbm] * 7,
+        out_specs=(vmem, vmem, smem, smem, smem),
         scratch_shapes=[
             pltpu.VMEM((group, comps, (rows + 2 * SUB) * per, LANES), jnp.float32),
             pltpu.VMEM((rows + 2 * SUB, LANES), jnp.float32),
@@ -478,22 +517,24 @@
             pltpu.VMEM((half + 1, share + 2 * SUB, LANES), jnp.float32),
             pltpu.VMEM((ring, steps, LANES), jnp.float32),
             pltpu.VMEM((group, steps, LANES), jnp.float32),
+            pltpu.VMEM((group * comps * per, LANES), jnp.float32),
+            pltpu.VMEM((group * comps * per, LANES), jnp.float32),
             pltpu.SemaphoreType.REGULAR((3,)),
-            dma((4,)),
-            dma((chunks + 1,)),
+            dma((7,)),
+            dma,
             dma((chunks + 1,)),
             dma((3,)),
             dma((3,)),
+            dma,
             dma((chunks,)),
+            dma,
             dma((chunks,)),
-            dma((chunks,)),
-            dma((chunks,)),
-            dma((chunks,)),
-            dma((chunks,)),
-            dma((ring,)),
-            dma((ring,)),
-            dma((3,)),
-            dma((group,)),
+            dma,
+            dma,
+            dma,
+            dma,
+            dma,
+            dma,
         ],
         compiler_params=pltpu.CompilerParams(
             has_side_effects=True, collective_id=0, vmem_limit_bytes=VMEM_LIMIT
@@ -501,6 +542,8 @@
         name="sweep",
     )(
         keep(vol_curve),
+        keep(bucket),
+        keep(bump_size),
         keep(payoff.reshape(rows, LANES)),
         keep(positions.reshape(rows, LANES)),
         keep(offsets),
@@ -515,11 +558,16 @@
             jax.ShapeDtypeStruct((1, curves), jnp.float32),
         ),
         in_specs=[smem, smem, smem, vmem, vmem],
-        out_specs=(pl.BlockSpec(memory_space=pl.ANY), vmem),
-        scratch_shapes=[pltpu.VMEM((groups * rows * SUB, LANES), jnp.float32), dma((parts, groups))],
+        out_specs=(pl.BlockSpec(memory_space=pl.ANY), pl.BlockSpec(memory_space=pl.ANY)),
+        scratch_shapes=[
+            pltpu.VMEM((groups * rows * SUB, LANES), jnp.float32),
+            pltpu.VMEM((1, curves), jnp.float32),
+            dma((parts, groups)),
+            dma,
+        ],
         compiler_params=pltpu.CompilerParams(vmem_limit_bytes=VMEM_LIMIT),
         name="spread",
-    )(keep(vol_curve), keep(bucket), keep(bump_size), moved, sums)
+    )(vol_on, bucket_on, bump_on, moved, sums)
     bumped = bumped.reshape(groups, rows, SUB, LANES).transpose(0, 2, 1, 3).reshape(curves, nodes)
     return bumped, vega.reshape(curves)
 

time: 32.1 us -> 27.4 us (0.85)
  Pallas kernels: 31.1 us -> 26.3 us
    pallas_call x1, Pallas kernels: 28.4 us -> 24.8 us  [on_device(): pl.pallas_call(functools.partial(sweep_kernel, (n, nx, ny, steps, per, bl...]
    pallas_call x1, Pallas kernels: 2.7 us -> 1.53 us  [on_device(): pl.pallas_call(spread_kernel, out_shape=(jax.ShapeDtypeStruct((groups * r...]
where the time goes in v4:
time: 27.4 us; the launch traced here: 27 us
  Pallas kernels  26.3 us (96%)
  between operations  0.64 us (2%)
    pallas_call x1, Pallas kernels, on_device(): pl.pallas_call(functools.partial(sweep_kernel, (n, nx, ny, steps, per, bl...  24.8 us
    pallas_call x1, Pallas kernels, on_device(): pl.pallas_call(spread_kernel, out_shape=(jax.ShapeDtypeStruct((groups * r...  1.53 us

profile of v4, /device:TPU:5, one launch (start us, length us, event | category | flops | bytes accessed | tf_op | source)
XLA Modules:
  0.0 27.0 jit_solution(1718219461135752865)
XLA Ops:
  0.6 24.8 %sweep.1 = (f32[9,256,128]{2,1,0:T(8,128)S(1)}, f32[8,128]{1,0:T(8,128)S(1)}, f32[8]{0:T(128)S(4)}, s32[16]{0:T(128)S(4)}, f32[16]{0:T(128)S(4)}) custom-call(f32[8]{0:T(128)} %curve_ref.1, s32[16]{0:T(128)} %bucket_ref.1, f32[16]{0:T(128)} %bump_ref.1, f32[256,128]{1,0:T(8,128)} %bitcast.16, f32[256,128]{1,0:T(8,128)} %bitcast.17, s32[8,128]{1,0:T(8,128)} %offsets_ref.1, ...), custom_call_target="tpu_custom_call" | custom-call | tf_op jit(solution)/shard_map/sweep/pallas_call | solution.py:499
  25.5 1.5 %spread.1 = (f32[4096,128]{1,0:T(8,128)}, f32[1,16]{1,0:T(1,128)}) custom-call(f32[8]{0:T(128)S(4)} %get-tuple-element.9.vol_ref, s32[16]{0:T(128)S(4)} %get-tuple-element.10.bucket_ref, f32[16]{0:T(128)S(4)} %get-tuple-element.11.bump_ref, f32[9,256,128]{2,1,0:T(8,128)S(1)} %get-tuple-element.12.rows_ref, f32[8,128]{1,0:T(8,128)S(1)} %get-tuple-element.13.sums_ref), custom_call_target="tpu_custom_call" | custom-call | tf_op jit(solution)/shard_map/spread/pallas_call | solution.py:554

commit v5 on v4

--- a/solution.py
+++ b/solution.py
@@ -98,15 +98,22 @@
         begin = (start_of(c, a, b) + c * share) * per
         return pl.ds(pl.multiple_of(begin, SUB * per), (b - a) * per)
 
-    whole = slice(SUB * per, (SUB + rows) * per)
+    reach = bounds[1] + 2 * SUB
+
+    def table_load(i, a, b):
+        there = tab.at[core, :, (SUB + a) * per : (SUB + b) * per]
+        return pltpu.make_async_copy(tables_ref.at[:, a * per : b * per], there, loc_sem.at[i])
+
     loads = [
-        pltpu.make_async_copy(tables_ref, tab.at[core, :, whole], loc_sem.at[0]),
+        table_load(0, share - reach, share + reach),
         pltpu.make_async_copy(payoff_ref, pay.at[SUB : SUB + rows], loc_sem.at[1]),
         pltpu.make_async_copy(positions_ref, pos, loc_sem.at[2]),
         pltpu.make_async_copy(offsets_ref, offs.at[0], loc_sem.at[3]),
         pltpu.make_async_copy(curve_ref, vol_ref, loc_sem.at[4]),
         pltpu.make_async_copy(bucket_ref, picks_ref, loc_sem.at[5]),
         pltpu.make_async_copy(bump_ref, sizes_ref, loc_sem.at[6]),
+        table_load(7, 0, share - reach),
+        table_load(8, share + reach, rows),
     ]
 
     barrier = pltpu.get_barrier_semaphore()
@@ -114,38 +121,48 @@
     def greet(sem, to):
         pl.semaphore_signal(sem, inc=1, device_id=to, device_id_type=MESH)
 
-    keeper = jnp.logical_and(lower, first)
-    link = jnp.logical_and(upper, first)
     rest = jnp.logical_not(first)
 
-    @pl.when(link)
+    for copy in loads[:1] + loads[3:5]:
+        copy.start()
+
+    @pl.when(first)
     def _():
         greet(barrier, sibling)
-        greet(barrier, at(ring, 0))
-        greet(barrier, at(left, 0))
-
-    @pl.when(jnp.logical_and(upper, rest))
-    def _():
-        greet(barrier, at(ring, 0))
-        greet(barrier, at(right, 0))
+        greet(barrier, at(left, group))
+
+    @pl.when(rest)
+    def _():
+        greet(barrier, at(right, group))
+
+    @pl.when(upper)
+    def _():
+        greet(barrier, at(ring, 1))
+        loads[1].start()
+
+    for copy in loads[7:]:
+        copy.start()
 
     @pl.when(lower)
     def _():
-        greet(barrier, at(ring, group))
         for i in range(1, ring_size):
             greet(barrier, at(lax.rem(ring + i, ring_size), 0))
-
-    @pl.when(keeper)
-    def _():
-        greet(barrier, sibling)
-
-    for copy in loads:
+        loads[2].start()
+
+    for copy in loads[5:7]:
         copy.start()
 
-    @pl.when(rest)
+    @pl.when(jnp.logical_and(upper, rest))
     def _():
         pl.semaphore_wait(barrier, 1)
         greet(hello.at[0], sibling)
+
+    @pl.when(jnp.logical_and(lower, rest))
+    def _():
+        pl.semaphore_wait(barrier, 3)
+        greet(hello.at[0], sibling)
+        greet(hello.at[1], across)
+        greet(hello.at[1], diagonal)
 
     @pl.when(first)
     def _():
@@ -171,7 +188,10 @@
     there = tab.at[core, :, pl.ds(edge, SUB * per)]
     table_copies.append(remote(there, there, tab_send, tab_recv.at[chunks], sibling))
     order = [j for j, (lo, hi) in enumerate(pieces) if lo < hi] + [chunks]
-    for j in order:
+    table_copies[0].start()
+    loads[7].wait()
+    loads[8].wait()
+    for j in order[1:]:
         table_copies[j].start()
 
     def arrived(j):
@@ -320,7 +340,18 @@
                 prepare(*pieces[j], 0)
             if j == chunks - 1:
                 gather_edge()
-                pl.semaphore_wait(hello.at[2], 1)
+
+                @pl.when(first)
+                def _():
+                    pl.semaphore_wait(barrier, 4)
+                    greet(hello.at[2], sibling)
+                    greet(hello.at[2], across)
+                    greet(hello.at[2], diagonal)
+
+                @pl.when(rest)
+                def _():
+                    pl.semaphore_wait(hello.at[2], 1)
+
                 for copy in halo_copies:
                     copy.start()
                 for copy in halo_copies:
@@ -334,16 +365,7 @@
             for i, g in enumerate(passed):
                 mid[i, local(lo, hi), :] = state[g, pl.ds(shift, hi - lo), :]
             if j == 0:
-
-                @pl.when(first)
-                def _():
-                    pl.semaphore_wait(barrier, 2)
-                    greet(hello.at[1], sibling)
-
-                @pl.when(rest)
-                def _():
-                    pl.semaphore_wait(hello.at[1], 1)
-
+                pl.semaphore_wait(hello.at[1], 1)
             mid_copy(j).start()
         for copy in halo_copies:
             copy.wait_send()
@@ -364,22 +386,8 @@
         for j in range(chunks):
             lo, hi = bounds[j], bounds[j + 1]
             begin, end = lo - SUB, hi + SUB
-            if j == 1:
-
-                @pl.when(first)
-                def _():
-                    pl.semaphore_wait(barrier, 2 * ring_size + 2)
-                    greet(hello.at[2], sibling)
-                    greet(hello.at[2], across)
-                    greet(hello.at[2], diagonal)
-
             if j == 2:
-
-                @pl.when(rest)
-                def _():
-                    pl.semaphore_wait(hello.at[2], 1)
-
-            if j == 2:
+                pl.semaphore_wait(hello.at[2], 1)
                 for copy in halo_copies[1:]:
                     copy.start()
             if j == chunks - 1:
@@ -404,6 +412,16 @@
                     part[ring, g - 1 : g, :] = weighted
             far_copy(j).start()
             near_copy(j).start()
+
+        @pl.when(first)
+        def _():
+            pl.semaphore_wait(barrier, 2 * ring_size - 2)
+            greet(hello.at[3], sibling)
+
+        @pl.when(rest)
+        def _():
+            pl.semaphore_wait(hello.at[3], 1)
+
         for i in range(1, ring_size):
             own = part.at[ring]
             remote(own, own, ring_send, ring_recv, at(lax.rem(ring + i, ring_size), me)).start()
@@ -425,15 +443,6 @@
     all_of(tab.at[core, :, 0 : (share + 2 * SUB) * per], tab_send)
     loads[5].wait()
     loads[6].wait()
-
-    @pl.when(upper)
-    def _():
-        loads[2].wait()
-
-    @pl.when(lower)
-    def _():
-        loads[1].wait()
-
 
 def spread_kernel(
     vol_ref, bucket_ref, bump_ref, rows_ref, sums_ref, out_ref, vega_ref, held, small, sem, small_sem
@@ -483,7 +492,7 @@
     share = rows // group
     half = steps // 2
     ring = nx * ny
-    bounds = [share * k // (16 * SUB) * SUB for k in (0, 2, 5, 9, 13, 16)]
+    bounds = [share * k // (16 * SUB) * SUB for k in (0, 1, 3, 6, 10, 13, 16)]
     chunks = len(bounds) - 1
     widest = max(b - a for a, b in zip(bounds, bounds[1:])) + 3 * SUB
     tiles = tables.transpose(1, 0, 2).reshape(comps, per, rows, LANES).transpose(0, 2, 1, 3)
@@ -519,8 +528,8 @@
             pltpu.VMEM((group, steps, LANES), jnp.float32),
             pltpu.VMEM((group * comps * per, LANES), jnp.float32),
             pltpu.VMEM((group * comps * per, LANES), jnp.float32),
-            pltpu.SemaphoreType.REGULAR((3,)),
-            dma((7,)),
+            pltpu.SemaphoreType.REGULAR((4,)),
+            dma((9,)),
             dma,
             dma((chunks + 1,)),
             dma((3,)),

time: 27.4 us -> 25.7 us (0.938)
  Pallas kernels: 26.3 us -> 24.9 us
    pallas_call x1, Pallas kernels: 24.8 us -> 23.3 us  [on_device(): pl.pallas_call(functools.partial(sweep_kernel, (n, nx, ny, steps, per, bl...]
where the time goes in v5:
time: 25.7 us; the launch traced here: 25.5 us
  Pallas kernels  24.9 us (97%)
  between operations  0.64 us (2%)
    pallas_call x1, Pallas kernels, on_device(): pl.pallas_call(functools.partial(sweep_kernel, (n, nx, ny, steps, per, bl...  23.3 us
    pallas_call x1, Pallas kernels, on_device(): pl.pallas_call(spread_kernel, out_shape=(jax.ShapeDtypeStruct((groups * r...  1.53 us

profile of v5, /device:TPU:5, one launch (start us, length us, event | category | flops | bytes accessed | tf_op | source)
XLA Modules:
  0.0 25.5 jit_solution(12832485423814617583)
XLA Ops:
  0.6 23.3 %sweep.1 = (f32[9,256,128]{2,1,0:T(8,128)S(1)}, f32[8,128]{1,0:T(8,128)S(1)}, f32[8]{0:T(128)S(4)}, s32[16]{0:T(128)S(4)}, f32[16]{0:T(128)S(4)}) custom-call(f32[8]{0:T(128)} %curve_ref.1, s32[16]{0:T(128)} %bucket_ref.1, f32[16]{0:T(128)} %bump_ref.1, f32[256,128]{1,0:T(8,128)} %bitcast.16, f32[256,128]{1,0:T(8,128)} %bitcast.17, s32[8,128]{1,0:T(8,128)} %offsets_ref.1, ...), custom_call_target="tpu_custom_call" | custom-call | tf_op jit(solution)/shard_map/sweep/pallas_call | solution.py:508
  24.0 1.5 %spread.1 = (f32[4096,128]{1,0:T(8,128)}, f32[1,16]{1,0:T(1,128)}) custom-call(f32[8]{0:T(128)S(4)} %get-tuple-element.9.vol_ref, s32[16]{0:T(128)S(4)} %get-tuple-element.10.bucket_ref, f32[16]{0:T(128)S(4)} %get-tuple-element.11.bump_ref, f32[9,256,128]{2,1,0:T(8,128)S(1)} %get-tuple-element.12.rows_ref, f32[8,128]{1,0:T(8,128)S(1)} %get-tuple-element.13.sums_ref), custom_call_target="tpu_custom_call" | custom-call | tf_op jit(solution)/shard_map/spread/pallas_call | solution.py:563

commit v6 on v5

--- a/solution.py
+++ b/solution.py
@@ -22,6 +22,7 @@
     positions_ref,
     offsets_ref,
     tables_ref,
+    lines_ref,
     rows_ref,
     sums_ref,
     vol_ref,
@@ -35,11 +36,16 @@
     state,
     mid,
     part,
-    tot,
+    gathered,
+    strip_sum,
+    total,
     edge_out,
     edge_in,
+    lent,
     hello,
     loc_sem,
+    lent_send,
+    lent_recv,
     tab_send,
     tab_recv,
     halo_send,
@@ -52,10 +58,12 @@
     near_recv,
     ring_send,
     ring_recv,
+    strip_send,
+    strip_recv,
     tot_send,
     tot_recv,
 ):
-    n, nx, ny, steps, per, block_len, bounds = dims
+    n, nx, ny, steps, per, block_len, bounds, strip = dims
     ring_size = nx * ny
     rows = payoff_ref.shape[0]
     blocks = offsets_ref.shape[1]
@@ -139,6 +147,7 @@
     def _():
         greet(barrier, at(ring, 1))
         loads[1].start()
+        loads[2].start()
 
     for copy in loads[7:]:
         copy.start()
@@ -178,6 +187,23 @@
     def fresh(j):
         lo = -SUB if j == 0 else min(bounds[j] + 2 * SUB, share)
         return lo, min(bounds[j + 1] + 2 * SUB, share)
+
+    from_row, to_row = bounds[strip], bounds[strip + 1]
+    lent_rows = to_row - from_row + 2
+
+    def lend(c, to):
+        begin = c * share + jnp.where(c == 0, share - to_row, from_row) - 1
+        source = lines_ref.at[:, pl.ds(begin, lent_rows)]
+        there = lent.at[core, :, SUB - 1 : SUB - 1 + lent_rows]
+        return remote(source, there, lent_send, lent_recv, to)
+
+    @pl.when(lower)
+    def _():
+        lend(core, across).start()
+        lend(1 - core, diagonal).start()
+
+    def all_of(ref, sem):
+        pltpu.make_async_copy(ref, ref, sem).wait()
 
     table_copies = []
     pieces = [fresh(j) for j in range(chunks)]
@@ -243,14 +269,14 @@
     loads[3].wait()
     loads[4].wait()
 
-    def prepare(a, b, source):
+    def prepare(a, b, source, borrowed=False):
         count = b - a
         begin = start_of(core, a, b)
         row = lax.broadcasted_iota(jnp.int32, (count, blocks), 0) + (begin - SUB + core * share + rows)
         hit = lax.broadcasted_iota(jnp.int32, (count, blocks), 1) == lax.rem(row, rows) * LANES // block_len
         here = pl.ds(begin, count)
         for t in range(half):
-            step = side * half + t
+            step = t if borrowed else side * half + t
             slot, at_step = t // per, t % per
             line = offs[source, pl.ds(step, 1), :].astype(jnp.float32)
             branch = jnp.sum(jnp.where(hit, line, 0.0), axis=1, keepdims=True)
@@ -259,6 +285,8 @@
             high = branch > 0.5
 
             def entry(k):
+                if borrowed:
+                    return lent[slot, k, 0:count, at_step, :]
                 first_row = (begin + core * share) * per + at_step
                 return tab[slot, k, pl.ds(first_row, count, stride=per), :]
 
@@ -307,10 +335,21 @@
     def mid_piece(j):
         return (-SUB if j == 0 else bounds[j] + SUB), bounds[j + 1] + SUB
 
-    def mid_copy(j):
-        lo, hi = mid_piece(j)
-        here = mid.at[:, local(lo, hi)]
+    def mid_copy(j, c):
+        lo = -1 if j == 0 else bounds[j] + 1
+        hi = bounds[j + 1] + 1
+        begin = SUB + (share - hi if c == 0 else lo)
+        here = mid.at[:, begin : begin + hi - lo]
         return remote(here, here, mid_send, mid_recv.at[j], across)
+
+    def each_core(act):
+        @pl.when(first)
+        def _():
+            act(0)
+
+        @pl.when(rest)
+        def _():
+            act(1)
 
     def result_at(c, j):
         return rows_ref.at[:, owned_at(c, bounds[j], bounds[j + 1])]
@@ -323,11 +362,42 @@
         here = result_at(core, j)
         return remote(here, here, near_send, near_recv, sibling)
 
-    def all_of(ref, sem):
-        pltpu.make_async_copy(ref, ref, sem).wait()
+    def weigh(g, here, fresh):
+        weighted = jnp.sum(pos[here, :] * rows_ref[g, here, :], axis=0, keepdims=True)
+        part[g - 1 : g, :] = weighted if fresh else part[g - 1 : g, :] + weighted
+
+    def packed():
+        each = jnp.broadcast_to(jnp.sum(part[...], axis=1, keepdims=True), (steps, LANES))
+        place = lax.broadcasted_iota(jnp.int32, (steps, LANES), 0)
+        lane = lax.broadcasted_iota(jnp.int32, (steps, LANES), 1)
+        return jnp.sum(jnp.where(place == lane, each, 0.0), axis=0, keepdims=True)
+
+    strip_copy = remote(strip_sum.at[0], strip_sum.at[1], strip_send, strip_recv, across)
+    def total_copy(to):
+        return remote(total.at[0], total.at[1], tot_send, tot_recv, to)
+
 
     mine = rows_ref.at[:, owned_at(core, 0, share)]
     others = rows_ref.at[:, owned_at(1 - core, 0, share)]
+
+    wrapped = lax.axis_index("ny") == 0
+
+    def send_halos():
+        gather_edge()
+
+        @pl.when(first)
+        def _():
+            pl.semaphore_wait(barrier, 4)
+            greet(hello.at[2], sibling)
+            greet(hello.at[2], across)
+            greet(hello.at[2], diagonal)
+
+        @pl.when(rest)
+        def _():
+            pl.semaphore_wait(hello.at[2], 1)
+
+        for copy in halo_copies:
+            copy.start()
 
     @pl.when(upper)
     def _():
@@ -339,21 +409,7 @@
                 arrived(j).wait_recv()
                 prepare(*pieces[j], 0)
             if j == chunks - 1:
-                gather_edge()
-
-                @pl.when(first)
-                def _():
-                    pl.semaphore_wait(barrier, 4)
-                    greet(hello.at[2], sibling)
-                    greet(hello.at[2], across)
-                    greet(hello.at[2], diagonal)
-
-                @pl.when(rest)
-                def _():
-                    pl.semaphore_wait(hello.at[2], 1)
-
-                for copy in halo_copies:
-                    copy.start()
+                pl.when(wrapped)(send_halos)
                 for copy in halo_copies:
                     copy.wait_recv()
                 place_edge()
@@ -366,14 +422,35 @@
                 mid[i, local(lo, hi), :] = state[g, pl.ds(shift, hi - lo), :]
             if j == 0:
                 pl.semaphore_wait(hello.at[1], 1)
-            mid_copy(j).start()
+            each_core(lambda c: mid_copy(j, c).start())
+            if j == 1:
+                pl.when(jnp.logical_not(wrapped))(send_halos)
+        loads[2].wait()
+        all_of(lent.at[:, :, SUB - 1 : SUB - 1 + lent_rows], lent_recv)
+        begin, end = from_row - SUB, to_row + SUB
+        prepare(begin, end, 0, True)
+        for i, g in enumerate(passed):
+            state[g, 0 : end - begin, :] = mid[i, local(begin, end), :]
+        advance(begin, end, 0)
+        for g in range(steps + 1):
+            rows_ref[g, owned_at(core, from_row, to_row), :] = state[g, SUB : end - begin - SUB, :]
+            if g:
+                weigh(g, owned_at(core, from_row, to_row), True)
+        strip_sum[0] = packed()
+        strip_copy.start()
+        far_copy(strip).start()
+        near_copy(strip).start()
         for copy in halo_copies:
             copy.wait_send()
         for j in range(chunks):
-            far_copy(j).wait_recv()
-            near_copy(j).start()
-        all_of(tot, tot_recv)
-        all_of(mid, mid_send)
+            if j != strip:
+                far_copy(j).wait_recv()
+                near_copy(j).start()
+        total_copy(across).wait_recv()
+        sums_ref[...] = total[1]
+        strip_copy.wait_send()
+        all_of(mid.at[:, 0 : share + 2], mid_send)
+        far_copy(strip).wait_send()
 
     @pl.when(lower)
     def _():
@@ -386,58 +463,79 @@
         for j in range(chunks):
             lo, hi = bounds[j], bounds[j + 1]
             begin, end = lo - SUB, hi + SUB
-            if j == 2:
+            if j == 0:
                 pl.semaphore_wait(hello.at[2], 1)
                 for copy in halo_copies[1:]:
                     copy.start()
+            if j == strip:
+                mid_copy(j, 0).wait_recv()
+
+                @pl.when(first)
+                def _():
+                    pl.semaphore_wait(barrier, 2 * ring_size - 2)
+                    greet(hello.at[3], sibling)
+
+                continue
             if j == chunks - 1:
                 for copy in halo_copies[1:]:
                     copy.wait_recv()
                 place_edge()
                 prepare(share, share + SUB, 1)
-            mid_copy(j).wait_recv()
+            mid_copy(j, 0).wait_recv()
             count = end - begin
-            for i, g in enumerate(passed):
-                state[g, 0:count, :] = mid[i, local(begin, end), :]
+
+            def take(c):
+                skip = SUB - 1
+                start = share - hi if c == 0 else lo
+                a, b = (skip, count) if c == 0 else (0, count - skip)
+                for i, g in enumerate(passed):
+                    state[g, a:b, :] = mid[i, start + a : start + b, :]
+
+            each_core(take)
             advance(begin, end, 0)
             here = owned_at(core, lo, hi)
-            weights = pos[here, :]
             for g in range(steps + 1):
-                center = state[g, SUB : SUB + hi - lo, :]
-                rows_ref[g, here, :] = center
-                if g:
-                    weighted = jnp.sum(weights * center, axis=0, keepdims=True)
-                    if j:
-                        weighted = weighted + part[ring, g - 1 : g, :]
-                    part[ring, g - 1 : g, :] = weighted
+                rows_ref[g, here, :] = state[g, SUB : SUB + hi - lo, :]
             far_copy(j).start()
             near_copy(j).start()
-
-        @pl.when(first)
-        def _():
-            pl.semaphore_wait(barrier, 2 * ring_size - 2)
-            greet(hello.at[3], sibling)
+            for g in range(1, steps + 1):
+                weigh(g, here, j == 0)
+
+        strip_copy.wait_recv()
+        own = core * ring_size + ring
+        gathered[own] = packed() + strip_sum[1]
 
         @pl.when(rest)
         def _():
             pl.semaphore_wait(hello.at[3], 1)
 
         for i in range(1, ring_size):
-            own = part.at[ring]
-            remote(own, own, ring_send, ring_recv, at(lax.rem(ring + i, ring_size), me)).start()
-        all_of(part.at[1:ring_size], ring_recv)
-        tot[core] = jnp.sum(part[...], axis=0)
-        total = tot.at[core]
-        for to in (sibling, across, diagonal):
-            remote(total, total, tot_send, tot_recv, to).start()
-        all_of(tot.at[1 - core], tot_recv)
-        all_of(part.at[1:ring_size], ring_send)
-        all_of(pay.at[0 : 3 * steps], tot_send)
+            for c in range(group):
+                to = at(lax.rem(ring + i, ring_size), c)
+                remote(gathered.at[own], gathered.at[own], ring_send, ring_recv, to).start()
+        remote(gathered.at[own], gathered.at[own], ring_send, ring_recv, sibling).start()
+        far_copy(strip).wait_recv()
+        near_copy(strip).start()
+        all_of(gathered.at[1 : group * ring_size], ring_recv)
+        total[0] = jnp.sum(gathered[...], axis=0)
+
+        @pl.when(rest)
+        def _():
+            total_copy(across).start()
+            total_copy(diagonal).start()
+
+        sums_ref[...] = total[0]
+        all_of(gathered.at[1 : group * ring_size], ring_send)
+
+        @pl.when(rest)
+        def _():
+            all_of(gathered.at[0:2], tot_send)
+
         for copy in halo_copies[1:]:
             copy.wait_send()
-        all_of(mine, far_send)
-
-    sums_ref[...] = jnp.sum(tot[...], axis=0)
+        all_of(rows_ref.at[:, owned_at(core, 0, share - (to_row - from_row))], far_send)
+        all_of(lent.at[:, :, SUB - 1 : SUB - 1 + lent_rows], lent_send)
+
     all_of(others, near_recv)
     all_of(mine, near_send)
     all_of(tab.at[core, :, 0 : (share + 2 * SUB) * per], tab_send)
@@ -458,10 +556,11 @@
         slope = 2.0 * vol_ref[s] + bump_ref[b]
         picks.append((s, slope, bump_ref[b] * slope))
     lane = lax.broadcasted_iota(jnp.int32, (1, curves), 1)
+    spot = lax.broadcasted_iota(jnp.int32, (1, LANES), 1)
     total = jnp.zeros((1, curves), jnp.float32)
     for b in range(curves):
         s, slope, _ = picks[b]
-        weighted = jnp.sum(sums_ref[pl.ds(s, 1), :], axis=1, keepdims=True)
+        weighted = jnp.sum(jnp.where(spot == s, sums_ref[...], 0.0), axis=1, keepdims=True)
         total = jnp.where(lane == b, slope * weighted, total)
     small[...] = total
     copies = [pltpu.make_async_copy(small, vega_ref, small_sem)]
@@ -492,11 +591,12 @@
     share = rows // group
     half = steps // 2
     ring = nx * ny
-    bounds = [share * k // (16 * SUB) * SUB for k in (0, 1, 3, 6, 10, 13, 16)]
+    bounds = [share * k // (16 * SUB) * SUB for k in (0, 1, 3, 6, 10, 12, 16)]
+    strip = 4
     chunks = len(bounds) - 1
     widest = max(b - a for a, b in zip(bounds, bounds[1:])) + 3 * SUB
-    tiles = tables.transpose(1, 0, 2).reshape(comps, per, rows, LANES).transpose(0, 2, 1, 3)
-    tiles = tiles.reshape(comps, rows * per, LANES)
+    lines = tables.transpose(1, 0, 2).reshape(comps, per, rows, LANES).transpose(0, 2, 1, 3)
+    tiles = lines.reshape(comps, rows * per, LANES)
     dma = pltpu.SemaphoreType.DMA
     vmem = pl.BlockSpec(memory_space=pltpu.VMEM)
     smem = pl.BlockSpec(memory_space=pltpu.SMEM)
@@ -506,15 +606,15 @@
         return pltpu.with_memory_space_constraint(x, pltpu.HBM)
 
     moved, sums, vol_on, bucket_on, bump_on = pl.pallas_call(
-        functools.partial(sweep_kernel, (n, nx, ny, steps, per, block_len, bounds)),
+        functools.partial(sweep_kernel, (n, nx, ny, steps, per, block_len, bounds, strip)),
         out_shape=(
             pltpu.VMEM((steps + 1, rows, LANES), jnp.float32),
-            pltpu.VMEM((steps, LANES), jnp.float32),
+            pltpu.VMEM((1, LANES), jnp.float32),
             pltpu.SMEM(vol_curve.shape, vol_curve.dtype),
             pltpu.SMEM(bucket.shape, bucket.dtype),
             pltpu.SMEM(bump_size.shape, bump_size.dtype),
         ),
-        in_specs=[hbm] * 7,
+        in_specs=[hbm] * 8,
         out_specs=(vmem, vmem, smem, smem, smem),
         scratch_shapes=[
             pltpu.VMEM((group, comps, (rows + 2 * SUB) * per, LANES), jnp.float32),
@@ -524,12 +624,19 @@
             pltpu.VMEM((half, 10, share + 2 * SUB, LANES), jnp.float32),
             pltpu.VMEM((steps + 1, widest, LANES), jnp.float32),
             pltpu.VMEM((half + 1, share + 2 * SUB, LANES), jnp.float32),
-            pltpu.VMEM((ring, steps, LANES), jnp.float32),
-            pltpu.VMEM((group, steps, LANES), jnp.float32),
+            pltpu.VMEM((steps, LANES), jnp.float32),
+            pltpu.VMEM((group * ring, 1, LANES), jnp.float32),
+            pltpu.VMEM((2, 1, LANES), jnp.float32),
+            pltpu.VMEM((2, 1, LANES), jnp.float32),
             pltpu.VMEM((group * comps * per, LANES), jnp.float32),
             pltpu.VMEM((group * comps * per, LANES), jnp.float32),
+            pltpu.VMEM(
+                (group, comps, bounds[strip + 1] - bounds[strip] + 2 * SUB, per, LANES), jnp.float32
+            ),
             pltpu.SemaphoreType.REGULAR((4,)),
             dma((9,)),
+            dma,
+            dma,
             dma,
             dma((chunks + 1,)),
             dma((3,)),
@@ -538,6 +645,8 @@
             dma((chunks,)),
             dma,
             dma((chunks,)),
+            dma,
+            dma,
             dma,
             dma,
             dma,
@@ -557,6 +666,7 @@
         keep(positions.reshape(rows, LANES)),
         keep(offsets),
         keep(tiles),
+        keep(lines),
     )
     groups = curves // SUB
     parts = max(1, rows // (4 * SUB))

time: 25.7 us -> 23.8 us (0.926)
  the two profiles are of different devices: /device:TPU:5 before, /device:TPU:1 now
where the time goes in v6:
time: 23.8 us; the launch traced here: 23.6 us
  Pallas kernels  23 us (97%)
  between operations  0.64 us (3%)
    pallas_call x1, Pallas kernels, on_device(): pl.pallas_call(functools.partial(sweep_kernel, (n, nx, ny, steps, per, bl...  21.4 us
    pallas_call x1, Pallas kernels, on_device(): pl.pallas_call(spread_kernel, out_shape=(jax.ShapeDtypeStruct((groups * r...  1.54 us

profile of v6, /device:TPU:1, one launch (start us, length us, event | category | flops | bytes accessed | tf_op | source)
XLA Modules:
  0.0 23.6 jit_solution(3816730807269143629)
XLA Ops:
  0.6 21.4 %sweep.1 = (f32[9,256,128]{2,1,0:T(8,128)S(1)}, f32[1,128]{1,0:T(1,128)S(1)}, f32[8]{0:T(128)S(4)}, s32[16]{0:T(128)S(4)}, f32[16]{0:T(128)S(4)}) custom-call(f32[8]{0:T(128)} %curve_ref.1, s32[16]{0:T(128)} %bucket_ref.1, f32[16]{0:T(128)} %bump_ref.1, f32[256,128]{1,0:T(8,128)} %bitcast.17, f32[256,128]{1,0:T(8,128)} %bitcast.18, s32[8,128]{1,0:T(8,128)} %offsets_ref.1, ...), custom_call_target="tpu_custom_call" | custom-call | tf_op jit(solution)/shard_map/sweep/pallas_call | solution.py:608
  22.1 1.5 %spread.1 = (f32[4096,128]{1,0:T(8,128)}, f32[1,16]{1,0:T(1,128)}) custom-call(f32[8]{0:T(128)S(4)} %get-tuple-element.9.vol_ref, s32[16]{0:T(128)S(4)} %get-tuple-element.10.bucket_ref, f32[16]{0:T(128)S(4)} %get-tuple-element.11.bump_ref, f32[9,256,128]{2,1,0:T(8,128)S(1)} %get-tuple-element.12.rows_ref, f32[1,128]{1,0:T(1,128)S(1)} %get-tuple-element.13.sums_ref), custom_call_target="tpu_custom_call" | custom-call | tf_op jit(solution)/shard_map/spread/pallas_call | solution.py:673

commit v7 on v6

--- a/solution.py
+++ b/solution.py
@@ -22,7 +22,6 @@
     positions_ref,
     offsets_ref,
     tables_ref,
-    lines_ref,
     rows_ref,
     sums_ref,
     vol_ref,
@@ -191,38 +190,41 @@
     from_row, to_row = bounds[strip], bounds[strip + 1]
     lent_rows = to_row - from_row + 2
 
-    def lend(c, to):
-        begin = c * share + jnp.where(c == 0, share - to_row, from_row) - 1
-        source = lines_ref.at[:, pl.ds(begin, lent_rows)]
-        there = lent.at[core, :, SUB - 1 : SUB - 1 + lent_rows]
-        return remote(source, there, lent_send, lent_recv, to)
-
-    @pl.when(lower)
-    def _():
-        lend(core, across).start()
-        lend(1 - core, diagonal).start()
+    lent_at = slice((SUB - 1) * per, (SUB - 1 + lent_rows) * per)
+
+    def lend(c):
+        begin = SUB + c * share + (share - to_row if c == 0 else from_row) - 1
+        source = tab.at[core, :, begin * per : (begin + lent_rows) * per]
+        to = at(ring, (1 - side) * group + c)
+        return remote(source, lent.at[core, :, lent_at], lent_send, lent_recv, to)
 
     def all_of(ref, sem):
         pltpu.make_async_copy(ref, ref, sem).wait()
 
+    pieces = [fresh(j) for j in range(chunks)]
+    parts = [pieces[0], (pieces[1][0], pieces[2][1]), (pieces[3][0], share)]
+    needed = {0: 0, 1: 1, 3: 2}
     table_copies = []
-    pieces = [fresh(j) for j in range(chunks)]
-    for j, (lo, hi) in enumerate(pieces):
+    for j, (lo, hi) in enumerate(parts):
         there = tab.at[core, :, table_at(1 - core, lo, hi)]
         table_copies.append(remote(there, there, tab_send, tab_recv.at[j], sibling))
     edge = pl.multiple_of(jnp.where(first, SUB, rows) * per, SUB * per)
     there = tab.at[core, :, pl.ds(edge, SUB * per)]
-    table_copies.append(remote(there, there, tab_send, tab_recv.at[chunks], sibling))
-    order = [j for j, (lo, hi) in enumerate(pieces) if lo < hi] + [chunks]
+    table_copies.append(remote(there, there, tab_send, tab_recv.at[3], sibling))
     table_copies[0].start()
     loads[7].wait()
     loads[8].wait()
-    for j in order[1:]:
-        table_copies[j].start()
+
+    @pl.when(lower)
+    def _():
+        for c in range(group):
+            lend(c).start()
+
+    for copy in table_copies[1:]:
+        copy.start()
 
     def arrived(j):
-        lo, hi = pieces[j]
-        here = tab.at[1 - core, :, table_at(core, lo, hi)]
+        here = tab.at[1 - core, :, table_at(core, *parts[j])]
         return remote(here, here, tab_send, tab_recv.at[j], sibling)
 
     out_from = pl.multiple_of(jnp.where(first, rows, SUB), SUB)
@@ -240,7 +242,7 @@
 
     def gather_edge():
         taken = tab.at[1 - core, :, pl.ds(pl.multiple_of(out_from * per, SUB * per), SUB * per)]
-        remote(taken, taken, tab_send, tab_recv.at[chunks], sibling).wait_recv()
+        remote(taken, taken, tab_send, tab_recv.at[3], sibling).wait_recv()
 
         @pl.when(first)
         def _():
@@ -286,7 +288,7 @@
 
             def entry(k):
                 if borrowed:
-                    return lent[slot, k, 0:count, at_step, :]
+                    return lent[slot, k, pl.ds(at_step, count, stride=per), :]
                 first_row = (begin + core * share) * per + at_step
                 return tab[slot, k, pl.ds(first_row, count, stride=per), :]
 
@@ -335,9 +337,15 @@
     def mid_piece(j):
         return (-SUB if j == 0 else bounds[j] + SUB), bounds[j + 1] + SUB
 
-    def mid_copy(j, c):
+    def mid_rows(j):
         lo = -1 if j == 0 else bounds[j] + 1
         hi = bounds[j + 1] + 1
+        return (hi - 2 if j == strip else lo), hi
+
+    mid_total = sum(hi - lo for lo, hi in map(mid_rows, range(chunks)))
+
+    def mid_copy(j, c):
+        lo, hi = mid_rows(j)
         begin = SUB + (share - hi if c == 0 else lo)
         here = mid.at[:, begin : begin + hi - lo]
         return remote(here, here, mid_send, mid_recv.at[j], across)
@@ -399,14 +407,20 @@
         for copy in halo_copies:
             copy.start()
 
+    def send_lower_halos():
+        pl.semaphore_wait(hello.at[2], 1)
+        for copy in halo_copies[1:]:
+            copy.start()
+
     @pl.when(upper)
     def _():
         loads[1].wait()
         for j in range(chunks):
             lo, hi = mid_piece(j)
             begin, end = max(lo - SUB, -SUB), min(hi + SUB, share + SUB)
+            if j in needed:
+                arrived(needed[j]).wait_recv()
             if pieces[j][0] < pieces[j][1]:
-                arrived(j).wait_recv()
                 prepare(*pieces[j], 0)
             if j == chunks - 1:
                 pl.when(wrapped)(send_halos)
@@ -426,7 +440,7 @@
             if j == 1:
                 pl.when(jnp.logical_not(wrapped))(send_halos)
         loads[2].wait()
-        all_of(lent.at[:, :, SUB - 1 : SUB - 1 + lent_rows], lent_recv)
+        all_of(lent.at[:, :, lent_at], lent_recv)
         begin, end = from_row - SUB, to_row + SUB
         prepare(begin, end, 0, True)
         for i, g in enumerate(passed):
@@ -449,7 +463,7 @@
         total_copy(across).wait_recv()
         sums_ref[...] = total[1]
         strip_copy.wait_send()
-        all_of(mid.at[:, 0 : share + 2], mid_send)
+        all_of(mid.at[:, 0:mid_total], mid_send)
         far_copy(strip).wait_send()
 
     @pl.when(lower)
@@ -457,16 +471,17 @@
         loads[2].wait()
         gather_edge()
         for j in range(chunks):
+            if j in needed:
+                arrived(needed[j]).wait_recv()
             if pieces[j][0] < pieces[j][1]:
-                arrived(j).wait_recv()
                 prepare(*pieces[j], 0)
         for j in range(chunks):
             lo, hi = bounds[j], bounds[j + 1]
             begin, end = lo - SUB, hi + SUB
             if j == 0:
-                pl.semaphore_wait(hello.at[2], 1)
-                for copy in halo_copies[1:]:
-                    copy.start()
+                pl.when(jnp.logical_not(wrapped))(send_lower_halos)
+            if j == 2:
+                pl.when(wrapped)(send_lower_halos)
             if j == strip:
                 mid_copy(j, 0).wait_recv()
 
@@ -534,7 +549,7 @@
         for copy in halo_copies[1:]:
             copy.wait_send()
         all_of(rows_ref.at[:, owned_at(core, 0, share - (to_row - from_row))], far_send)
-        all_of(lent.at[:, :, SUB - 1 : SUB - 1 + lent_rows], lent_send)
+        all_of(lent.at[:, :, lent_at], lent_send)
 
     all_of(others, near_recv)
     all_of(mine, near_send)
@@ -548,23 +563,13 @@
     curves = bucket_ref.shape[0]
     groups = curves // SUB
     rows = rows_ref.shape[1]
-    parts = sem.shape[0]
+    parts = max(1, rows // (4 * SUB))
     span = rows // parts
     picks = []
     for b in range(curves):
         s = bucket_ref[b]
         slope = 2.0 * vol_ref[s] + bump_ref[b]
         picks.append((s, slope, bump_ref[b] * slope))
-    lane = lax.broadcasted_iota(jnp.int32, (1, curves), 1)
-    spot = lax.broadcasted_iota(jnp.int32, (1, LANES), 1)
-    total = jnp.zeros((1, curves), jnp.float32)
-    for b in range(curves):
-        s, slope, _ = picks[b]
-        weighted = jnp.sum(jnp.where(spot == s, sums_ref[...], 0.0), axis=1, keepdims=True)
-        total = jnp.where(lane == b, slope * weighted, total)
-    small[...] = total
-    copies = [pltpu.make_async_copy(small, vega_ref, small_sem)]
-    copies[0].start()
     for i in range(parts):
         here = slice(i * span, (i + 1) * span)
         base = rows_ref[0, here, :]
@@ -574,11 +579,20 @@
             held[pl.ds(line, span, stride=SUB), :] = base + change * rows_ref[s + 1, here, :]
         for g in range(groups):
             place = slice((g * rows + i * span) * SUB, (g * rows + (i + 1) * span) * SUB)
-            copy = pltpu.make_async_copy(held.at[place], out_ref.at[place], sem.at[i, g])
-            copy.start()
-            copies.append(copy)
-    for copy in copies:
-        copy.wait()
+            pltpu.make_async_copy(held.at[place], out_ref.at[place], sem).start()
+        if i == 0:
+            lane = lax.broadcasted_iota(jnp.int32, (1, curves), 1)
+            spot = lax.broadcasted_iota(jnp.int32, (1, LANES), 1)
+            total = jnp.zeros((1, curves), jnp.float32)
+            for b in range(curves):
+                s, slope, _ = picks[b]
+                weighted = jnp.sum(jnp.where(spot == s, sums_ref[...], 0.0), axis=1, keepdims=True)
+                total = jnp.where(lane == b, slope * weighted, total)
+            small[...] = total
+            vega_copy = pltpu.make_async_copy(small, vega_ref, small_sem)
+            vega_copy.start()
+    vega_copy.wait()
+    pltpu.make_async_copy(held, out_ref, sem).wait()
 
 
 def on_device(n, nx, ny, payoff, positions, tables, offsets, vol_curve, bucket, bump_size):
@@ -591,12 +605,12 @@
     share = rows // group
     half = steps // 2
     ring = nx * ny
-    bounds = [share * k // (16 * SUB) * SUB for k in (0, 1, 3, 6, 10, 12, 16)]
+    bounds = [share * k // (16 * SUB) * SUB for k in (0, 1, 3, 6, 10, 12, 14, 16)]
     strip = 4
     chunks = len(bounds) - 1
     widest = max(b - a for a, b in zip(bounds, bounds[1:])) + 3 * SUB
-    lines = tables.transpose(1, 0, 2).reshape(comps, per, rows, LANES).transpose(0, 2, 1, 3)
-    tiles = lines.reshape(comps, rows * per, LANES)
+    tiles = tables.transpose(1, 0, 2).reshape(comps, per, rows, LANES).transpose(0, 2, 1, 3)
+    tiles = tiles.reshape(comps, rows * per, LANES)
     dma = pltpu.SemaphoreType.DMA
     vmem = pl.BlockSpec(memory_space=pltpu.VMEM)
     smem = pl.BlockSpec(memory_space=pltpu.SMEM)
@@ -614,7 +628,7 @@
             pltpu.SMEM(bucket.shape, bucket.dtype),
             pltpu.SMEM(bump_size.shape, bump_size.dtype),
         ),
-        in_specs=[hbm] * 8,
+        in_specs=[hbm] * 7,
         out_specs=(vmem, vmem, smem, smem, smem),
         scratch_shapes=[
             pltpu.VMEM((group, comps, (rows + 2 * SUB) * per, LANES), jnp.float32),
@@ -631,14 +645,14 @@
             pltpu.VMEM((group * comps * per, LANES), jnp.float32),
             pltpu.VMEM((group * comps * per, LANES), jnp.float32),
             pltpu.VMEM(
-                (group, comps, bounds[strip + 1] - bounds[strip] + 2 * SUB, per, LANES), jnp.float32
+                (group, comps, (bounds[strip + 1] - bounds[strip] + 2 * SUB) * per, LANES), jnp.float32
             ),
             pltpu.SemaphoreType.REGULAR((4,)),
             dma((9,)),
             dma,
             dma,
             dma,
-            dma((chunks + 1,)),
+            dma((4,)),
             dma((3,)),
             dma((3,)),
             dma,
@@ -666,10 +680,8 @@
         keep(positions.reshape(rows, LANES)),
         keep(offsets),
         keep(tiles),
-        keep(lines),
     )
     groups = curves // SUB
-    parts = max(1, rows // (4 * SUB))
     bumped, vega = pl.pallas_call(
         spread_kernel,
         out_shape=(
@@ -681,7 +693,7 @@
         scratch_shapes=[
             pltpu.VMEM((groups * rows * SUB, LANES), jnp.float32),
             pltpu.VMEM((1, curves), jnp.float32),
-            dma((parts, groups)),
+            dma,
             dma,
         ],
         compiler_params=pltpu.CompilerParams(vmem_limit_bytes=VMEM_LIMIT),

time: 23.8 us -> 23.1 us (0.971)
  the two profiles are of different devices: /device:TPU:1 before, /device:TPU:5 now
where the time goes in v7:
time: 23.1 us; the launch traced here: 22.9 us
  Pallas kernels  22.3 us (97%)
  between operations  0.64 us (3%)
    pallas_call x1, Pallas kernels, on_device(): pl.pallas_call(functools.partial(sweep_kernel, (n, nx, ny, steps, per, bl...  20.9 us
    pallas_call x1, Pallas kernels, on_device(): pl.pallas_call(spread_kernel, out_shape=(jax.ShapeDtypeStruct((groups * r...  1.4 us

profile of v7, /device:TPU:5, one launch (start us, length us, event | category | flops | bytes accessed | tf_op | source)
XLA Modules:
  0.0 22.9 jit_solution(5043566063028608889)
XLA Ops:
  0.6 20.9 %sweep.1 = (f32[9,256,128]{2,1,0:T(8,128)S(1)}, f32[1,128]{1,0:T(1,128)S(1)}, f32[8]{0:T(128)S(4)}, s32[16]{0:T(128)S(4)}, f32[16]{0:T(128)S(4)}) custom-call(f32[8]{0:T(128)} %curve_ref.1, s32[16]{0:T(128)} %bucket_ref.1, f32[16]{0:T(128)} %bump_ref.1, f32[256,128]{1,0:T(8,128)} %bitcast.16, f32[256,128]{1,0:T(8,128)} %bitcast.17, s32[8,128]{1,0:T(8,128)} %offsets_ref.1, ...), custom_call_target="tpu_custom_call" | custom-call | tf_op jit(solution)/shard_map/sweep/pallas_call | solution.py:622
  21.5 1.4 %spread.1 = (f32[4096,128]{1,0:T(8,128)}, f32[1,16]{1,0:T(1,128)}) custom-call(f32[8]{0:T(128)S(4)} %get-tuple-element.9.vol_ref, s32[16]{0:T(128)S(4)} %get-tuple-element.10.bucket_ref, f32[16]{0:T(128)S(4)} %get-tuple-element.11.bump_ref, f32[9,256,128]{2,1,0:T(8,128)S(1)} %get-tuple-element.12.rows_ref, f32[1,128]{1,0:T(1,128)S(1)} %get-tuple-element.13.sums_ref), custom_call_target="tpu_custom_call" | custom-call | tf_op jit(solution)/shard_map/spread/pallas_call | solution.py:685

commit v8 on v7

--- a/solution.py
+++ b/solution.py
@@ -43,24 +43,20 @@
     lent,
     hello,
     loc_sem,
-    lent_send,
-    lent_recv,
+    lent_sem,
     tab_send,
     tab_recv,
     halo_send,
     halo_recv,
     mid_send,
-    mid_recv,
     far_send,
-    far_recv,
+    cross_recv,
     near_send,
     near_recv,
     ring_send,
     ring_recv,
-    strip_send,
-    strip_recv,
-    tot_send,
-    tot_recv,
+    sum_send,
+    sum_recv,
 ):
     n, nx, ny, steps, per, block_len, bounds, strip = dims
     ring_size = nx * ny
@@ -120,7 +116,7 @@
         pltpu.make_async_copy(bucket_ref, picks_ref, loc_sem.at[5]),
         pltpu.make_async_copy(bump_ref, sizes_ref, loc_sem.at[6]),
         table_load(7, 0, share - reach),
-        table_load(8, share + reach, rows),
+        table_load(7, share + reach, rows),
     ]
 
     barrier = pltpu.get_barrier_semaphore()
@@ -196,7 +192,7 @@
         begin = SUB + c * share + (share - to_row if c == 0 else from_row) - 1
         source = tab.at[core, :, begin * per : (begin + lent_rows) * per]
         to = at(ring, (1 - side) * group + c)
-        return remote(source, lent.at[core, :, lent_at], lent_send, lent_recv, to)
+        return remote(source, lent.at[core, :, lent_at], lent_sem, lent_sem, to)
 
     def all_of(ref, sem):
         pltpu.make_async_copy(ref, ref, sem).wait()
@@ -212,8 +208,7 @@
     there = tab.at[core, :, pl.ds(edge, SUB * per)]
     table_copies.append(remote(there, there, tab_send, tab_recv.at[3], sibling))
     table_copies[0].start()
-    loads[7].wait()
-    loads[8].wait()
+    all_of(tab.at[core, :, 0 : (rows - 2 * reach) * per], loc_sem.at[7])
 
     @pl.when(lower)
     def _():
@@ -232,10 +227,10 @@
     halo_copies = [
         remote(
             pay.at[pl.ds(out_from, SUB)], pay.at[pl.ds(out_to, SUB)],
-            halo_send.at[0], halo_recv.at[0], outer,
+            halo_send, halo_recv.at[0], outer,
         ),
-        remote(offs.at[0], offs.at[1], halo_send.at[1], halo_recv.at[1], outer),
-        remote(edge_out, edge_in, halo_send.at[2], halo_recv.at[2], outer),
+        remote(offs.at[0], offs.at[1], halo_send, halo_recv.at[1], outer),
+        remote(edge_out, edge_in, halo_send, halo_recv.at[2], outer),
     ]
 
     lines = [(slot, k, (slot * comps + k) * per) for slot in range(group) for k in range(comps)]
@@ -338,17 +333,17 @@
         return (-SUB if j == 0 else bounds[j] + SUB), bounds[j + 1] + SUB
 
     def mid_rows(j):
-        lo = -1 if j == 0 else bounds[j] + 1
-        hi = bounds[j + 1] + 1
-        return (hi - 2 if j == strip else lo), hi
-
-    mid_total = sum(hi - lo for lo, hi in map(mid_rows, range(chunks)))
+        lo = -1 if j == 0 else bounds[j] - 1 if j == strip + 1 else bounds[j] + 1
+        return lo, bounds[j + 1] + 1
+
+    sent = [j for j in range(chunks) if j != strip]
+    mid_total = sum(hi - lo for lo, hi in map(mid_rows, sent))
 
     def mid_copy(j, c):
         lo, hi = mid_rows(j)
         begin = SUB + (share - hi if c == 0 else lo)
         here = mid.at[:, begin : begin + hi - lo]
-        return remote(here, here, mid_send, mid_recv.at[j], across)
+        return remote(here, here, mid_send, cross_recv.at[j], across)
 
     def each_core(act):
         @pl.when(first)
@@ -364,7 +359,7 @@
 
     def far_copy(j):
         here = result_at(core, j)
-        return remote(here, here, far_send, far_recv.at[j], across)
+        return remote(here, here, far_send, cross_recv.at[j], across)
 
     def near_copy(j):
         here = result_at(core, j)
@@ -380,15 +375,16 @@
         lane = lax.broadcasted_iota(jnp.int32, (steps, LANES), 1)
         return jnp.sum(jnp.where(place == lane, each, 0.0), axis=0, keepdims=True)
 
-    strip_copy = remote(strip_sum.at[0], strip_sum.at[1], strip_send, strip_recv, across)
+    strip_copy = remote(strip_sum.at[0], strip_sum.at[1], sum_send, sum_recv, across)
     def total_copy(to):
-        return remote(total.at[0], total.at[1], tot_send, tot_recv, to)
+        return remote(total.at[0], total.at[1], sum_send, sum_recv, to)
 
 
     mine = rows_ref.at[:, owned_at(core, 0, share)]
     others = rows_ref.at[:, owned_at(1 - core, 0, share)]
 
     wrapped = lax.axis_index("ny") == 0
+    halo_rows = steps * blocks // LANES + group * comps * per
 
     def send_halos():
         gather_edge()
@@ -436,11 +432,12 @@
                 mid[i, local(lo, hi), :] = state[g, pl.ds(shift, hi - lo), :]
             if j == 0:
                 pl.semaphore_wait(hello.at[1], 1)
-            each_core(lambda c: mid_copy(j, c).start())
+            if j != strip:
+                each_core(lambda c: mid_copy(j, c).start())
             if j == 1:
                 pl.when(jnp.logical_not(wrapped))(send_halos)
         loads[2].wait()
-        all_of(lent.at[:, :, lent_at], lent_recv)
+        all_of(lent.at[:, :, lent_at], lent_sem)
         begin, end = from_row - SUB, to_row + SUB
         prepare(begin, end, 0, True)
         for i, g in enumerate(passed):
@@ -454,8 +451,7 @@
         strip_copy.start()
         far_copy(strip).start()
         near_copy(strip).start()
-        for copy in halo_copies:
-            copy.wait_send()
+        all_of(pay.at[0 : SUB + halo_rows], halo_send)
         for j in range(chunks):
             if j != strip:
                 far_copy(j).wait_recv()
@@ -483,12 +479,11 @@
             if j == 2:
                 pl.when(wrapped)(send_lower_halos)
             if j == strip:
-                mid_copy(j, 0).wait_recv()
 
                 @pl.when(first)
                 def _():
                     pl.semaphore_wait(barrier, 2 * ring_size - 2)
-                    greet(hello.at[3], sibling)
+                    greet(hello.at[1], sibling)
 
                 continue
             if j == chunks - 1:
@@ -522,7 +517,7 @@
 
         @pl.when(rest)
         def _():
-            pl.semaphore_wait(hello.at[3], 1)
+            pl.semaphore_wait(hello.at[1], 1)
 
         for i in range(1, ring_size):
             for c in range(group):
@@ -544,12 +539,11 @@
 
         @pl.when(rest)
         def _():
-            all_of(gathered.at[0:2], tot_send)
-
-        for copy in halo_copies[1:]:
-            copy.wait_send()
+            all_of(gathered.at[0:2], sum_send)
+
+        all_of(pay.at[0:halo_rows], halo_send)
         all_of(rows_ref.at[:, owned_at(core, 0, share - (to_row - from_row))], far_send)
-        all_of(lent.at[:, :, lent_at], lent_send)
+        all_of(lent.at[:, :, lent_at], lent_sem)
 
     all_of(others, near_recv)
     all_of(mine, near_send)
@@ -605,8 +599,8 @@
     share = rows // group
     half = steps // 2
     ring = nx * ny
-    bounds = [share * k // (16 * SUB) * SUB for k in (0, 1, 3, 6, 10, 12, 14, 16)]
-    strip = 4
+    bounds = [share * k // (16 * SUB) * SUB for k in (0, 1, 2, 4, 7, 10, 12, 14, 16)]
+    strip = 5
     chunks = len(bounds) - 1
     widest = max(b - a for a, b in zip(bounds, bounds[1:])) + 3 * SUB
     tiles = tables.transpose(1, 0, 2).reshape(comps, per, rows, LANES).transpose(0, 2, 1, 3)
@@ -647,20 +641,16 @@
             pltpu.VMEM(
                 (group, comps, (bounds[strip + 1] - bounds[strip] + 2 * SUB) * per, LANES), jnp.float32
             ),
-            pltpu.SemaphoreType.REGULAR((4,)),
-            dma((9,)),
-            dma,
+            pltpu.SemaphoreType.REGULAR((3,)),
+            dma((8,)),
             dma,
             dma,
             dma((4,)),
+            dma,
             dma((3,)),
-            dma((3,)),
+            dma,
             dma,
             dma((chunks,)),
-            dma,
-            dma((chunks,)),
-            dma,
-            dma,
             dma,
             dma,
             dma,

time: 23.1 us -> 22.9 us (level)
  no operation moved by 1% of the time
where the time goes in v8:
time: 22.9 us; the launch traced here: 22.7 us
  Pallas kernels  22.1 us (97%)
  between operations  0.64 us (3%)
    pallas_call x1, Pallas kernels, on_device(): pl.pallas_call(functools.partial(sweep_kernel, (n, nx, ny, steps, per, bl...  20.7 us
    pallas_call x1, Pallas kernels, on_device(): pl.pallas_call(spread_kernel, out_shape=(jax.ShapeDtypeStruct((groups * r...  1.4 us

profile of v8, /device:TPU:5, one launch (start us, length us, event | category | flops | bytes accessed | tf_op | source)
XLA Modules:
  0.0 22.7 jit_solution(4425671172479667984)
XLA Ops:
  0.6 20.7 %sweep.1 = (f32[9,256,128]{2,1,0:T(8,128)S(1)}, f32[1,128]{1,0:T(1,128)S(1)}, f32[8]{0:T(128)S(4)}, s32[16]{0:T(128)S(4)}, f32[16]{0:T(128)S(4)}) custom-call(f32[8]{0:T(128)} %curve_ref.1, s32[16]{0:T(128)} %bucket_ref.1, f32[16]{0:T(128)} %bump_ref.1, f32[256,128]{1,0:T(8,128)} %bitcast.16, f32[256,128]{1,0:T(8,128)} %bitcast.17, s32[8,128]{1,0:T(8,128)} %offsets_ref.1, ...), custom_call_target="tpu_custom_call" | custom-call | tf_op jit(solution)/shard_map/sweep/pallas_call | solution.py:616
  21.3 1.4 %spread.1 = (f32[4096,128]{1,0:T(8,128)}, f32[1,16]{1,0:T(1,128)}) custom-call(f32[8]{0:T(128)S(4)} %get-tuple-element.9.vol_ref, s32[16]{0:T(128)S(4)} %get-tuple-element.10.bucket_ref, f32[16]{0:T(128)S(4)} %get-tuple-element.11.bump_ref, f32[9,256,128]{2,1,0:T(8,128)S(1)} %get-tuple-element.12.rows_ref, f32[1,128]{1,0:T(1,128)S(1)} %get-tuple-element.13.sums_ref), custom_call_target="tpu_custom_call" | custom-call | tf_op jit(solution)/shard_map/spread/pallas_call | solution.py:675
